TPU v7x, 32 devices: a whole 2x2x4 slice. The times are simulated.
32 devices in a mesh: geo: 4 (over x, core), comp: 8 (over z, y).
Axes of the slice: x: 2, y: 2, z: 4, core: 2. Of those that a mesh axis runs over, the one named last changes fastest.
Arguments:
- spectrum: bfloat16 [1152, 512, 128], P('comp', 'geo'), may hold values from 0.049804688 to 1
- land_mask: int32 [512, 128], P('geo'), may hold values 0 or 1
- wind_speed: float32 [512, 128], P('geo'), may hold values from 0.5 to 2
- wind_dir: float32 [512, 128], P('geo'), may hold values from -3.140625 to 3.140625
- input_rate: float32 [1152], P('comp'), may hold values from 0.05 to 0.5
- dissipation: float32 [1152], replicated, may hold values from 0.05 to 0.5
- pair_first: bfloat16 [1728, 1152], replicated, may hold values from -0.1875 to 0.1875
- pair_second: bfloat16 [1728, 1152], replicated, may hold values from -0.1875 to 0.1875
- merge_weight: bfloat16 [1152, 1728], replicated, may hold values from -0.15625 to 0.15625
Outputs:
- spectrum_next: bfloat16 [1152, 512, 128], P('comp', 'geo')
All inputs are finite; a program needn't handle non-finite values. No bound on the sum of `land_mask` on one device may be relied on, other than what follows from the above.
Results may differ from a plain program's by a relative error of at most 0.0038.
Values may be sent and summed in bfloat16 or wider, within the bound.
A program may use at most 128 MiB of HBM per device.

v0:
```python
import functools
import math

import jax
import jax.numpy as jnp
from jax import lax
from jax.experimental import pallas as pl
from jax.experimental.pallas import tpu as pltpu
from jax.sharding import PartitionSpec as P

ND = 36
PROP_STEPS = 6
HALO = 8
SENDS = 3
RETURNS = 2
F32 = jnp.float32
BF16 = jnp.bfloat16
VMEM = pltpu.VMEM
SMEM = pltpu.SMEM


def edges(cells, axis_dim):
    count = lax.axis_size("geo")
    ends = count - 1
    size = cells.shape[axis_dim]
    head = lax.slice_in_dim(cells, 0, HALO, axis=axis_dim)
    tail = lax.slice_in_dim(cells, size - HALO, size, axis=axis_dim)
    lower = lax.ppermute(tail, "geo", [(i, i + 1) for i in range(ends)])
    upper = lax.ppermute(head, "geo", [(i + 1, i) for i in range(ends)])
    return lower, upper


def block_of(comps):
    return 16 if comps % 16 == 0 else comps


def stride_of(block):
    return -(-block // 8) * 8


def upwind(v, mask, coef, at):
    center, west, east, south, north = (coef[at + k] for k in range(5))
    rows = v.shape[0]
    moved = west * pltpu.roll(v, 1, 1) + east * pltpu.roll(v, v.shape[1] - 1, 1)
    moved = moved + south * pltpu.roll(v, 1, 0) + north * pltpu.roll(v, rows - 1, 0)
    return (center * v + moved) * mask


def prop_kernel(coef, lower, cells, upper, mask, density, outgoing, turned):
    block, rows, cols = cells.shape
    stride = stride_of(block)
    first = pl.program_id(0) * block

    def one(c, carry):
        v = jnp.concatenate(
            [lower[c].astype(F32), cells[c].astype(F32), upper[c].astype(F32)], axis=0
        )
        sea = mask[...]
        for _ in range(PROP_STEPS):
            v = upwind(v, sea, coef, (first + c) * 8)
        density[c] = v
        turned[pl.ds(c, rows, stride=stride), :] = v[HALO : HALO + rows]
        return carry

    lax.fori_loop(0, block, one, 0)

    def pack(r, carry):
        start = pl.multiple_of(r * stride, 8)
        outgoing[r] = turned[pl.ds(start, block), :].astype(BF16)
        return carry

    lax.fori_loop(0, rows, pack, 0, unroll=8)


def propagate(coef, lower, cells, upper, mask):
    comps, rows, cols = cells.shape
    block = block_of(comps)
    tall = rows + 2 * HALO
    return pl.pallas_call(
        prop_kernel,
        grid=(comps // block,),
        in_specs=[
            pl.BlockSpec(memory_space=SMEM),
            pl.BlockSpec((block, HALO, cols), lambda i: (i, 0, 0)),
            pl.BlockSpec((block, rows, cols), lambda i: (i, 0, 0)),
            pl.BlockSpec((block, HALO, cols), lambda i: (i, 0, 0)),
            pl.BlockSpec((tall, cols), lambda i: (0, 0)),
        ],
        out_specs=[
            pl.BlockSpec((block, tall, cols), lambda i: (i, 0, 0)),
            pl.BlockSpec((rows, block, cols), lambda i: (0, i, 0)),
        ],
        out_shape=[
            jax.ShapeDtypeStruct((comps, tall, cols), F32),
            jax.ShapeDtypeStruct((rows, comps, cols), BF16),
        ],
        scratch_shapes=[VMEM((rows * stride_of(block), cols), F32)],
        cost_estimate=pl.CostEstimate(
            flops=comps * tall * cols * 100,
            bytes_accessed=comps * tall * cols * 8,
            transcendentals=0,
        ),
        name="propagate",
    )(coef, lower, cells, upper, mask)


def point_kernel(sends, *refs):
    near, far = refs[:sends], refs[sends : 2 * sends]
    loss, first, second, merge, out, spectra, product = refs[2 * sends :]
    peers, _, part, cols = near[0].shape
    local = sends * part
    comps, terms = merge.shape
    for side, group in enumerate((near, far)):
        lanes = slice(side * cols, (side + 1) * cols)
        for k in range(sends):
            for s in range(peers):
                at = s * local + k * part
                spectra[at : at + part, lanes] = group[k][s, 0]
    tile = max(t for t in range(16, 600, 16) if terms % t == 0)

    def multiply(t, carry):
        rows = pl.ds(pl.multiple_of(t * tile, 16), tile)
        x = spectra[...]
        one = jnp.dot(first[rows, :], x, preferred_element_type=F32)
        two = jnp.dot(second[rows, :], x, preferred_element_type=F32)
        product[rows, :] = (one * two).astype(BF16)
        return carry

    lax.fori_loop(0, terms // tile, multiply, 0)
    energy = jnp.sum(spectra[...].astype(F32), axis=0, keepdims=True)
    root = jnp.sqrt(energy / comps + 1e-06)
    if peers == 1:
        step = max(t for t in range(16, 600, 16) if comps % t == 0)
        for d in range(0, comps, step):
            rows = slice(d, d + step)
            moved = jnp.dot(merge[rows, :], product[...], preferred_element_type=F32)
            total = moved - loss[rows, :] * root * spectra[rows, :].astype(F32)
            out[0, 0, rows] = total[:, :cols].astype(BF16)
            out[0, 1, rows] = total[:, cols:].astype(BF16)
        return
    share = max(g for g in range(1, peers + 1) if peers % g == 0 and g * local <= 600)
    for d in range(0, peers, share):
        rows = slice(d * local, (d + share) * local)
        moved = jnp.dot(merge[rows, :], product[...], preferred_element_type=F32)
        total = moved - loss[rows, :] * root * spectra[rows, :].astype(F32)
        for g in range(share):
            piece = total[g * local : (g + 1) * local].astype(BF16)
            out[d + g, 0] = piece[:, :cols]
            out[d + g, 1] = piece[:, cols:]


def point_terms(chunks, start, pairs, loss, first, second, merge):
    sends = len(chunks)
    peers, rows, part, cols = chunks[0].shape
    local = sends * part
    comps, terms = merge.shape
    whole = lambda shape: pl.BlockSpec(shape, lambda i: (0, 0))
    near = pl.BlockSpec((peers, 1, part, cols), lambda i: (0, start + i, 0, 0))
    far = pl.BlockSpec((peers, 1, part, cols), lambda i: (0, rows - 1 - start - i, 0, 0))
    return pl.pallas_call(
        functools.partial(point_kernel, sends),
        grid=(pairs,),
        in_specs=[near] * sends
        + [far] * sends
        + [whole((comps, 1)), whole((terms, comps)), whole((terms, comps)), whole((comps, terms))],
        out_specs=pl.BlockSpec((peers, 2, local, cols), lambda i: (0, i, 0, 0)),
        out_shape=jax.ShapeDtypeStruct((peers, 2 * pairs, local, cols), BF16),
        scratch_shapes=[VMEM((comps, 2 * cols), BF16), VMEM((terms, 2 * cols), BF16)],
        cost_estimate=pl.CostEstimate(
            flops=pairs * 12 * comps * terms * cols,
            bytes_accessed=6 * comps * terms + pairs * 8 * comps * cols,
            transcendentals=0,
        ),
        compiler_params=pltpu.CompilerParams(vmem_limit_bytes=60 * 1024 * 1024),
        name="points",
    )(*chunks, *chunks, loss, first, second, merge)


def final_kernel(returns, coef, density, low_inc, high_inc, wind, mask, *refs):
    incs = refs[:returns]
    out, turned = refs[returns:]
    block, rows, cols = out.shape
    peers, held = incs[0].shape[:2]
    band = rows // peers
    stride = stride_of(block)
    first = pl.program_id(0) * block

    def place(s, carry):
        for k in range(returns):
            for j in range(held):
                a = k * (held // 2) + j // 2
                row = a if j % 2 == 0 else band - 1 - a
                at = pl.multiple_of((s * band + row) * stride, 8)
                turned[pl.ds(at, block), :] = incs[k][s, j].astype(F32)
        return carry

    lax.fori_loop(0, peers, place, 0)

    def one(c, carry):
        at = (first + c) * 8
        inc = jnp.concatenate(
            [low_inc[c], turned[pl.ds(c, rows, stride=stride), :], high_inc[c]], axis=0
        )
        v = density[c]
        facing = jnp.maximum(coef[at + 6] * wind[1] + coef[at + 7] * wind[2], 0.0)
        growth = coef[at + 5] * wind[0] * facing * facing
        v = v + growth * v + inc
        v = upwind(v, mask[...], coef, at)
        out[c] = v[HALO : HALO + rows].astype(BF16)
        return carry

    lax.fori_loop(0, block, one, 0)


def finish(coef, density, low_inc, high_inc, wind, mask, incs, lead):
    local, tall, cols = density.shape
    rows = tall - 2 * HALO
    block = block_of(local)
    peers, held = incs[0].shape[:2]
    return pl.pallas_call(
        functools.partial(final_kernel, len(incs)),
        grid=(local // block,),
        in_specs=[
            pl.BlockSpec(memory_space=SMEM),
            pl.BlockSpec((block, tall, cols), lambda i: (i, 0, 0)),
            pl.BlockSpec((block, HALO, cols), lambda i: (i, 0, 0)),
            pl.BlockSpec((block, HALO, cols), lambda i: (i, 0, 0)),
            pl.BlockSpec((3, tall, cols), lambda i: (0, 0, 0)),
            pl.BlockSpec((tall, cols), lambda i: (0, 0)),
        ]
        + [pl.BlockSpec((peers, held, block, cols), lambda i: (0, 0, i, 0))] * len(incs),
        out_specs=pl.BlockSpec((block, rows, cols), lambda i: (i, 0, 0)),
        out_shape=jax.ShapeDtypeStruct((local, rows, cols), BF16),
        scratch_shapes=[VMEM((rows * stride_of(block), cols), F32)],
        name="finish",
    )(coef, density, low_inc, high_inc, wind, mask, *incs)


def body(spectrum, land_mask, wind_speed, wind_dir, input_rate, dissipation, pair_first, pair_second, merge_weight):
    local, rows, cols = spectrum.shape
    peers = lax.axis_size("comp")
    band = rows // peers
    ids = lax.axis_index("comp") * local + jnp.arange(local, dtype=jnp.int32)
    frequency = (ids // ND).astype(F32)
    heading = 2.0 * math.pi * (ids % ND).astype(F32) / ND
    courant = 0.7 * jnp.power(F32(1.1), -frequency)
    cos_h, sin_h = jnp.cos(heading), jnp.sin(heading)
    west, east = jnp.maximum(courant * cos_h, 0.0), jnp.maximum(-courant * cos_h, 0.0)
    south, north = jnp.maximum(courant * sin_h, 0.0), jnp.maximum(-courant * sin_h, 0.0)
    center = 1.0 - west - east - south - north
    coef = jnp.stack([center, west, east, south, north, input_rate, cos_h, sin_h], axis=1).reshape(-1)

    lower, upper = edges(spectrum, 1)
    fields = jnp.stack([wind_speed, jnp.cos(wind_dir), jnp.sin(wind_dir), land_mask.astype(F32)])
    low_f, high_f = edges(fields, 1)
    fields = jnp.concatenate([low_f, fields, high_f], axis=1)
    wind, mask = fields[:3], fields[3]

    whole_tiles = local % (16 * SENDS) == 0
    sends = SENDS if whole_tiles else 1
    part = local // sends
    density, chunks = [], []
    for k in range(sends):
        cut = slice(k * part, (k + 1) * part)
        d, out = propagate(coef[k * part * 8 : (k + 1) * part * 8], lower[cut], spectrum[cut], upper[cut], mask)
        density.append(d)
        out = out.reshape(peers, band, part, cols)
        chunks.append(lax.all_to_all(out, "comp", split_axis=0, concat_axis=0, tiled=True))
    density = jnp.concatenate(density, axis=0)

    loss = dissipation[:, None]
    if not whole_tiles:
        chunks = [c.transpose(1, 0, 2, 3).reshape(1, band, peers * local, cols) for c in chunks]
    returns = max(1, min(RETURNS, band // 2))
    pairs = band // 2 // returns
    incs = []
    for k in range(returns):
        inc = point_terms(chunks, k * pairs, pairs, loss, pair_first, pair_second, merge_weight)
        if not whole_tiles:
            inc = inc.reshape(2 * pairs, peers, local, cols).transpose(1, 0, 2, 3)
        incs.append(lax.all_to_all(inc, "comp", split_axis=0, concat_axis=0, tiled=True))
    count = lax.axis_size("geo")
    ends = count - 1
    low = lax.ppermute(incs[0][peers - 1, 1], "geo", [(i, i + 1) for i in range(ends)])
    high = lax.ppermute(incs[0][0, 0], "geo", [(i + 1, i) for i in range(ends)])
    low = jnp.pad(low.astype(F32)[:, None], ((0, 0), (HALO - 1, 0), (0, 0)))
    high = jnp.pad(high.astype(F32)[:, None], ((0, 0), (0, HALO - 1), (0, 0)))
    return finish(coef, density, low, high, wind, mask, incs, HALO)


def solution(mesh):
    placed = (P("comp", "geo", None), P("geo", None), P("geo", None), P("geo", None), P("comp"), P(), P(), P(), P())
    return jax.shard_map(
        body, mesh=mesh, in_specs=placed, out_specs=P("comp", "geo", None), check_vma=False
    )
```

profile of v0, /device:TPU:0, one launch (start us, length us, event | category | flops | bytes accessed | tf_op | source)
XLA Modules:
  0.0 343.7 jit_solution(4999712243572808370)
XLA Ops:
  0.0 1.1 fusion.6
  1.1 2.4 collective-permute-start
  3.5 1.3 collective-permute-start.1
  4.8 0.8 convert_bitcast_fusion
  5.7 1.1 cosine_bitcast_fusion
  7.5 1.3 collective-permute-start.3
  8.8 5.7 %collective-permute-start.2 = (f32[4,8,128]{2,1,0:T(8,128)S(1)}, f32[4,8,128]{2,1,0:T(8,128)S(1)}, u32[]{:S(2)}, u32[]{:S(2)}) collective-permute-start(f32[4,8,128]{2,1,0:T(8,128)S(1)} %get-tuple-element.30), channel_id=1, source_target_pairs={{0,8},{8,16},{16,24},{1,9},{9,17},{17,25},{2,10},{10,18},{18,26},{... | collective-permute-start | bytes 49160 | tf_op jit(solution)/shard_map/ppermute | solution.py:28
  14.8 4.8 %fusion.5 = (bf16[48,128,128]{2,1,0:T(8,128)(2,1)}, bf16[48,128,128]{2,1,0:T(8,128)(2,1)}, bf16[48,128,128]{2,1,0:T(8,128)(2,1)}) fusion(bf16[144,128,128]{2,1,0:T(8,128)(2,1)} %param.9), kind=kLoop, calls=%fused_computation.32 | loop fusion | bytes 9437184 | tf_op jit(solution)/shard_map/slice | solution.py:265
  22.6 31.8 %propagate.3 = (f32[48,144,128]{2,1,0:T(8,128)}, bf16[128,48,128]{2,1,0:T(8,128)(2,1)}) custom-call(f32[384]{0:T(512)} %slice.70.coef, bf16[48,8,128]{2,1,0:T(8,128)(2,1)} %get-tuple-element.27.lower, bf16[48,128,128]{2,1,0:T(8,128)(2,1)} %get-tuple-element.17.cells, bf16[48,8,128]{2,1,0:T(8,128)(2,1)} %get-tuple-element.24.upper, ...), custom_call_target="tpu_custom_call" | custom-call | flops 88473600 | bytes 7077888 | tf_op jit(solution)/shard_map/propagate/pallas_call | solution.py:79
  54.3 5.8 %all-to-all-start = ((bf16[8,16,48,128]{3,2,1,0:T(8,128)(2,1)}), bf16[8,16,48,128]{3,2,1,0:T(8,128)(2,1)S(1)}, u32[]{:S(2)}, u32[]{:S(2)}) async-start(bf16[8,16,48,128]{3,2,1,0:T(8,128)(2,1)} %bitcast.20), calls=%async_computation | async-start | bytes 3145728 | tf_op jit(solution)/shard_map/all_to_all | solution.py:268
  60.9 31.7 %propagate.4 = (f32[48,144,128]{2,1,0:T(8,128)}, bf16[128,48,128]{2,1,0:T(8,128)(2,1)}) custom-call(f32[384]{0:T(512)} %slice.80.coef, bf16[48,8,128]{2,1,0:T(8,128)(2,1)} %get-tuple-element.29.lower, bf16[48,128,128]{2,1,0:T(8,128)(2,1)} %get-tuple-element.19.cells, bf16[48,8,128]{2,1,0:T(8,128)(2,1)} %get-tuple-element.26.upper, ...), custom_call_target="tpu_custom_call" | custom-call | flops 88473600 | bytes 7077888 | tf_op jit(solution)/shard_map/propagate/pallas_call | solution.py:79
  92.6 5.9 %all-to-all-done.refs_0_.refs_3_ = bf16[8,16,48,128]{3,2,1,0:T(8,128)(2,1)S(1)} async-done(((bf16[8,16,48,128]{3,2,1,0:T(8,128)(2,1)}), bf16[8,16,48,128]{3,2,1,0:T(8,128)(2,1)S(1)}, u32[]{:S(2)}, u32[]{:S(2)}) %all-to-all-start) | async-done | bytes 1572896 | tf_op jit(solution)/shard_map/all_to_all | solution.py:268
  98.5 3.8 %all-to-all-start.1 = ((bf16[8,16,48,128]{3,2,1,0:T(8,128)(2,1)}), bf16[8,16,48,128]{3,2,1,0:T(8,128)(2,1)S(1)}, u32[]{:S(2)}, u32[]{:S(2)}) async-start(bf16[8,16,48,128]{3,2,1,0:T(8,128)(2,1)} %bitcast.19), calls=%async_computation.1 | async-start | bytes 3145728 | tf_op jit(solution)/shard_map/all_to_all | solution.py:268
  103.1 31.7 %propagate.5 = (f32[48,144,128]{2,1,0:T(8,128)}, bf16[128,48,128]{2,1,0:T(8,128)(2,1)}) custom-call(f32[384]{0:T(512)} %slice.85.coef, bf16[48,8,128]{2,1,0:T(8,128)(2,1)} %get-tuple-element.28.lower, bf16[48,128,128]{2,1,0:T(8,128)(2,1)} %get-tuple-element.18.cells, bf16[48,8,128]{2,1,0:T(8,128)(2,1)} %get-tuple-element.25.upper, ...), custom_call_target="tpu_custom_call" | custom-call | flops 88473600 | bytes 7077888 | tf_op jit(solution)/shard_map/propagate/pallas_call | solution.py:79
  134.8 5.1 %all-to-all-done.1.refs_1_.refs_4_ = bf16[8,16,48,128]{3,2,1,0:T(8,128)(2,1)S(1)} async-done(((bf16[8,16,48,128]{3,2,1,0:T(8,128)(2,1)}), bf16[8,16,48,128]{3,2,1,0:T(8,128)(2,1)S(1)}, u32[]{:S(2)}, u32[]{:S(2)}) %all-to-all-start.1) | async-done | bytes 1572896 | tf_op jit(solution)/shard_map/all_to_all | solution.py:268
  139.9 4.3 %all-to-all-start.2 = ((bf16[8,16,48,128]{3,2,1,0:T(8,128)(2,1)}), bf16[8,16,48,128]{3,2,1,0:T(8,128)(2,1)}, u32[]{:S(2)}, u32[]{:S(2)}) async-start(bf16[8,16,48,128]{3,2,1,0:T(8,128)(2,1)} %bitcast.21), calls=%async_computation.2 | async-start | bytes 3145728 | tf_op jit(solution)/shard_map/all_to_all | solution.py:268
  144.2 1.1 broadcast_in_dim.14.refs_6_
  145.3 6.3 %copy.19.refs_9_ = bf16[1152,1728]{1,0:T(8,128)(2,1)} copy(bf16[1152,1728]{0,1:T(8,128)(2,1)} %param.17) | data formatting | bytes 7962624 | tf_op args[8]
  151.6 29.3 %all-to-all-done.2.refs_2_.refs_5_ = bf16[8,16,48,128]{3,2,1,0:T(8,128)(2,1)} async-done(((bf16[8,16,48,128]{3,2,1,0:T(8,128)(2,1)}), bf16[8,16,48,128]{3,2,1,0:T(8,128)(2,1)}, u32[]{:S(2)}, u32[]{:S(2)}) %all-to-all-start.2) | async-done | bytes 1572896 | tf_op jit(solution)/shard_map/all_to_all | solution.py:268
  180.9 22.7 %points.2 = bf16[8,8,144,128]{3,2,1,0:T(8,128)(2,1)} custom-call(bf16[8,16,48,128]{3,2,1,0:T(8,128)(2,1)} %copy-done.1, bf16[8,16,48,128]{3,2,1,0:T(8,128)(2,1)} %copy-done.2, bf16[8,16,48,128]{3,2,1,0:T(8,128)(2,1)} %all-to-all-done.2.refs_2_.refs_5_, bf16[8,16,48,128]{3,2,1,0:T(8,128)(2,1)} %copy-done.1, bf16[8,16,48,128]{3,2,1,0:T(8,128)(2,1)} %copy-done.2, ...), custom_call_target="tpu_custom_call" | custom-call | flops 12230590464 | bytes 16662528 | tf_op jit(solution)/shard_map/points/pallas_call | solution.py:160
  203.6 3.6 %all-to-all-start.3 = ((bf16[8,8,144,128]{3,2,1,0:T(8,128)(2,1)}), bf16[8,8,144,128]{3,2,1,0:T(8,128)(2,1)S(1)}, u32[]{:S(2)}, u32[]{:S(2)}) async-start(bf16[8,8,144,128]{3,2,1,0:T(8,128)(2,1)} %points.2), calls=%async_computation.3 | async-start | bytes 4718592 | tf_op jit(solution)/shard_map/all_to_all | solution.py:281
  207.2 22.7 %points.3 = bf16[8,8,144,128]{3,2,1,0:T(8,128)(2,1)} custom-call(bf16[8,16,48,128]{3,2,1,0:T(8,128)(2,1)} %copy-done.1, bf16[8,16,48,128]{3,2,1,0:T(8,128)(2,1)} %copy-done.2, bf16[8,16,48,128]{3,2,1,0:T(8,128)(2,1)} %all-to-all-done.2.refs_2_.refs_5_, bf16[8,16,48,128]{3,2,1,0:T(8,128)(2,1)} %copy-done.1, bf16[8,16,48,128]{3,2,1,0:T(8,128)(2,1)} %copy-done.2, ...), custom_call_target="tpu_custom_call" | custom-call | flops 12230590464 | bytes 16662528 | tf_op jit(solution)/shard_map/points/pallas_call | solution.py:160
  229.9 31.3 %all-to-all-done.3.refs_0_ = bf16[8,8,144,128]{3,2,1,0:T(8,128)(2,1)S(1)} async-done(((bf16[8,8,144,128]{3,2,1,0:T(8,128)(2,1)}), bf16[8,8,144,128]{3,2,1,0:T(8,128)(2,1)S(1)}, u32[]{:S(2)}, u32[]{:S(2)}) %all-to-all-start.3) | async-done | bytes 2359328 | tf_op jit(solution)/shard_map/all_to_all | solution.py:281
  261.2 4.4 %all-to-all-start.4 = ((bf16[8,8,144,128]{3,2,1,0:T(8,128)(2,1)}), bf16[8,8,144,128]{3,2,1,0:T(8,128)(2,1)}, u32[]{:S(2)}, u32[]{:S(2)}) async-start(bf16[8,8,144,128]{3,2,1,0:T(8,128)(2,1)} %points.3), calls=%async_computation.4 | async-start | bytes 4718592 | tf_op jit(solution)/shard_map/all_to_all | solution.py:281
  267.1 1.3 collective-permute-start.4
  268.4 9.0 %pad_maximum_fusion.density = f32[144,144,128]{2,1,0:T(8,128)} fusion(f32[48,144,128]{2,1,0:T(8,128)} %get-tuple-element.13, f32[48,144,128]{2,1,0:T(8,128)} %get-tuple-element.12, f32[48,144,128]{2,1,0:T(8,128)} %get-tuple-element.11), kind=kLoop, calls=%fused_computation | loop fusion | flops 5308416 | bytes 21233664 | tf_op jit(solution)/shard_map/concatenate | solution.py:269
  277.4 1.3 collective-permute-start.5
  278.8 1.0 copy.22.low_inc
  279.8 0.8 collective-permute-done.5
  280.6 1.0 copy.23.high_inc
  281.6 37.4 %all-to-all-done.4.refs_1_ = bf16[8,8,144,128]{3,2,1,0:T(8,128)(2,1)} async-done(((bf16[8,8,144,128]{3,2,1,0:T(8,128)(2,1)}), bf16[8,8,144,128]{3,2,1,0:T(8,128)(2,1)}, u32[]{:S(2)}, u32[]{:S(2)}) %all-to-all-start.4) | async-done | bytes 2359328 | tf_op jit(solution)/shard_map/all_to_all | solution.py:281
  319.0 24.6 %finish.1 = bf16[144,128,128]{2,1,0:T(8,128)(2,1)} custom-call(f32[1152]{0:T(1024)} %reshape.127.coef, f32[144,144,128]{2,1,0:T(8,128)} %pad_maximum_fusion.density, f32[144,8,128]{2,1,0:T(8,128)} %copy.22.low_inc, f32[144,8,128]{2,1,0:T(8,128)} %copy.23.high_inc, f32[3,144,128]{2,1,0:T(8,128)} %pad_maximum_fusion.1.wind, ...), custom_call_target="tpu_custom_call" | custom-call | tf_op jit(solution)/shard_map/finish/pallas_call | solution.py:220
  (39 shorter events, 7.1 us)
Async XLA Ops:
  1.1 20.0 %collective-permute-start = (bf16[144,8,128]{2,1,0:T(8,128)(2,1)S(1)}, bf16[144,8,128]{2,1,0:T(8,128)(2,1)S(1)}, u32[]{:S(2)}, u32[]{:S(2)}) collective-permute-start(bf16[144,8,128]{2,1,0:T(8,128)(2,1)S(1)} %get-tuple-element.21), channel_id=1, source_target_pairs={{0,8},{8,16},{16,24},{1,9},{9,17},{17,25},{2,10},{10,18},{18,26},{... | collective-permute-start | bytes 884744 | tf_op jit(solution)/shard_map/ppermute | solution.py:28
  3.5 18.3 %collective-permute-start.1 = (bf16[144,8,128]{2,1,0:T(8,128)(2,1)S(1)}, bf16[144,8,128]{2,1,0:T(8,128)(2,1)S(1)}, u32[]{:S(2)}, u32[]{:S(2)}) collective-permute-start(bf16[144,8,128]{2,1,0:T(8,128)(2,1)S(1)} %get-tuple-element.20), channel_id=1, source_target_pairs={{8,0},{16,8},{24,16},{9,1},{17,9},{25,17},{10,2},{18,10},{26,18},{... | collective-permute-start | bytes 884744 | tf_op jit(solution)/shard_map/ppermute | solution.py:29
  7.5 13.0 %collective-permute-start.3 = (f32[4,8,128]{2,1,0:T(8,128)S(1)}, f32[4,8,128]{2,1,0:T(8,128)S(1)}, u32[]{:S(2)}, u32[]{:S(2)}) collective-permute-start(f32[4,8,128]{2,1,0:T(8,128)S(1)} %get-tuple-element.31), channel_id=1, source_target_pairs={{8,0},{16,8},{24,16},{9,1},{17,9},{25,17},{10,2},{18,10},{26,18},{... | collective-permute-start | bytes 49160 | tf_op jit(solution)/shard_map/ppermute | solution.py:29
  8.8 11.7 %collective-permute-start.2 = (f32[4,8,128]{2,1,0:T(8,128)S(1)}, f32[4,8,128]{2,1,0:T(8,128)S(1)}, u32[]{:S(2)}, u32[]{:S(2)}) collective-permute-start(f32[4,8,128]{2,1,0:T(8,128)S(1)} %get-tuple-element.30), channel_id=1, source_target_pairs={{0,8},{8,16},{16,24},{1,9},{9,17},{17,25},{2,10},{10,18},{18,26},{... | collective-permute-start | bytes 49160 | tf_op jit(solution)/shard_map/ppermute | solution.py:28
  14.8 4.8 %copy-start.5 = (f32[144]{0:T(256)S(1)}, f32[144]{0:T(256)}, u32[]{:S(2)}) copy-start(f32[144]{0:T(256)} %param.13) | copy-start | bytes 1732
  14.8 5.6 %copy-start.3 = (f32[128,128]{1,0:T(8,128)S(1)}, f32[128,128]{1,0:T(8,128)}, u32[]{:S(2)}) copy-start(f32[128,128]{1,0:T(8,128)} %param.11) | copy-start | bytes 196612
  54.3 44.2 %all-to-all-start = ((bf16[8,16,48,128]{3,2,1,0:T(8,128)(2,1)}), bf16[8,16,48,128]{3,2,1,0:T(8,128)(2,1)S(1)}, u32[]{:S(2)}, u32[]{:S(2)}) async-start(bf16[8,16,48,128]{3,2,1,0:T(8,128)(2,1)} %bitcast.20), calls=%async_computation | async-start | bytes 3145728 | tf_op jit(solution)/shard_map/all_to_all | solution.py:268
  98.5 41.4 %copy-start.1 = (bf16[8,16,48,128]{3,2,1,0:T(8,128)(2,1)}, bf16[8,16,48,128]{3,2,1,0:T(8,128)(2,1)S(1)}, u32[]{:S(2)}) copy-start(bf16[8,16,48,128]{3,2,1,0:T(8,128)(2,1)S(1)} %all-to-all-done.refs_0_.refs_3_) | copy-start | bytes 4718596
  98.5 45.7 %copy-start.4 = (f32[1152]{0:T(1024)S(1)}, f32[1152]{0:T(1024)}, u32[]{:S(2)}) copy-start(f32[1152]{0:T(1024)} %param.14) | copy-start | bytes 13828
  98.5 41.4 %all-to-all-start.1 = ((bf16[8,16,48,128]{3,2,1,0:T(8,128)(2,1)}), bf16[8,16,48,128]{3,2,1,0:T(8,128)(2,1)S(1)}, u32[]{:S(2)}, u32[]{:S(2)}) async-start(bf16[8,16,48,128]{3,2,1,0:T(8,128)(2,1)} %bitcast.19), calls=%async_computation.1 | async-start | bytes 3145728 | tf_op jit(solution)/shard_map/all_to_all | solution.py:268
  139.9 11.7 %copy-start.2 = (bf16[8,16,48,128]{3,2,1,0:T(8,128)(2,1)}, bf16[8,16,48,128]{3,2,1,0:T(8,128)(2,1)S(1)}, u32[]{:S(2)}) copy-start(bf16[8,16,48,128]{3,2,1,0:T(8,128)(2,1)S(1)} %all-to-all-done.1.refs_1_.refs_4_) | copy-start | bytes 4718596
  139.9 41.0 %all-to-all-start.2 = ((bf16[8,16,48,128]{3,2,1,0:T(8,128)(2,1)}), bf16[8,16,48,128]{3,2,1,0:T(8,128)(2,1)}, u32[]{:S(2)}, u32[]{:S(2)}) async-start(bf16[8,16,48,128]{3,2,1,0:T(8,128)(2,1)} %bitcast.21), calls=%async_computation.2 | async-start | bytes 3145728 | tf_op jit(solution)/shard_map/all_to_all | solution.py:268
  203.6 57.7 %all-to-all-start.3 = ((bf16[8,8,144,128]{3,2,1,0:T(8,128)(2,1)}), bf16[8,8,144,128]{3,2,1,0:T(8,128)(2,1)S(1)}, u32[]{:S(2)}, u32[]{:S(2)}) async-start(bf16[8,8,144,128]{3,2,1,0:T(8,128)(2,1)} %points.2), calls=%async_computation.3 | async-start | bytes 4718592 | tf_op jit(solution)/shard_map/all_to_all | solution.py:281
  261.2 16.2 %copy-start = (bf16[8,8,144,128]{3,2,1,0:T(8,128)(2,1)}, bf16[8,8,144,128]{3,2,1,0:T(8,128)(2,1)S(1)}, u32[]{:S(2)}) copy-start(bf16[8,8,144,128]{3,2,1,0:T(8,128)(2,1)S(1)} %all-to-all-done.3.refs_0_) | copy-start | bytes 7077892
  261.2 57.8 %all-to-all-start.4 = ((bf16[8,8,144,128]{3,2,1,0:T(8,128)(2,1)}), bf16[8,8,144,128]{3,2,1,0:T(8,128)(2,1)}, u32[]{:S(2)}, u32[]{:S(2)}) async-start(bf16[8,8,144,128]{3,2,1,0:T(8,128)(2,1)} %points.3), calls=%async_computation.4 | async-start | bytes 4718592 | tf_op jit(solution)/shard_map/all_to_all | solution.py:281
  267.1 11.6 %collective-permute-start.4 = (bf16[144,128]{1,0:T(8,128)(2,1)S(1)}, bf16[144,128]{1,0:T(8,128)(2,1)S(1)}, u32[]{:S(2)}, u32[]{:S(2)}) collective-permute-start(bf16[144,128]{1,0:T(8,128)(2,1)S(1)} %get-tuple-element.23), channel_id=1, source_target_pairs={{0,8},{8,16},{16,24},{1,9},{9,17},{17,25},{2,10},{10,18},{18,26},{... | collective-permute-start | bytes 110600 | tf_op jit(solution)/shard_map/ppermute | solution.py:284
  277.4 3.1 collective-permute-start.5
where the time goes:
time: 345 us; the launch traced here: 344 us
  Pallas kernels  165 us (48%)
  waiting for transfers between devices  110 us (32%)
  starting transfers between devices  35.2 us (10%)
  local copies, waits for them, and re-layouts  21 us (6%)
  other arithmetic  12.3 us (4%)
    pallas_call x3, Pallas kernels, propagate(): pl.pallas_call(prop_kernel, grid=(comps // block,), in_specs=[pl.BlockSpe...  95.2 us
    all_to_all x2, waiting for transfers between devices, body(): lax.all_to_all(inc, 'comp', split_axis=0, concat_axis=0, tiled=True)  68.7 us
    pallas_call x2, Pallas kernels, point_terms(): pl.pallas_call(functools.partial(point_kernel, sends), grid=(pairs,), in_...  45.4 us
    all_to_all x3, waiting for transfers between devices, body(): lax.all_to_all(out, 'comp', split_axis=0, concat_axis=0, tiled=True)  40.3 us
    pallas_call x1, Pallas kernels, finish(): pl.pallas_call(functools.partial(final_kernel, len(incs)), grid=(local //...  24.6 us
    all_to_all x3, starting transfers between devices, body(): lax.all_to_all(out, 'comp', split_axis=0, concat_axis=0, tiled=True)  14 us
    concatenate x1, other arithmetic, body(): density = jnp.concatenate(density, axis=0)  9.02 us
    ppermute x2, starting transfers between devices, edges(): lower = lax.ppermute(tail, 'geo', [(i, i + 1) for i in range(ends)])  8.15 us
  transfers between devices with their start and end apart: 11, of which 6 were waited for; matrix products, arithmetic and copies ran while one was open for 9% of the time, Pallas kernels for 25%

commit v1 on v0

--- a/solution.py
+++ b/solution.py
@@ -16,6 +16,12 @@
 F32 = jnp.float32
 BF16 = jnp.bfloat16
 VMEM = pltpu.VMEM
+ANY = pl.BlockSpec(memory_space=pl.ANY)
+WHOLE = pl.BlockSpec(memory_space=pltpu.VMEM)
+MESH = pl.DeviceIdType.MESH
+DMA = pltpu.SemaphoreType.DMA
+PAD = 16
+CHUNK = 2
 SMEM = pltpu.SMEM
 
 
@@ -236,7 +242,7 @@
     )(coef, density, low_inc, high_inc, wind, mask, *incs)
 
 
-def body(spectrum, land_mask, wind_speed, wind_dir, input_rate, dissipation, pair_first, pair_second, merge_weight):
+def plain_body(spectrum, land_mask, wind_speed, wind_dir, input_rate, dissipation, pair_first, pair_second, merge_weight):
     local, rows, cols = spectrum.shape
     peers = lax.axis_size("comp")
     band = rows // peers
@@ -288,6 +294,627 @@
     return finish(coef, density, low, high, wind, mask, incs, HALO)
 
 
+def geo_halo_kernel(spectrum, mask, speed, angle, near, near_mask, near_speed, near_angle, send, recv):
+    geo, ends = lax.axis_index("geo"), lax.axis_size("geo") - 1
+    rows = spectrum.shape[1]
+    barrier = pltpu.get_barrier_semaphore()
+    has_low, has_high = geo > 0, geo < ends
+
+    @pl.when(has_low)
+    def _():
+        pl.semaphore_signal(barrier, inc=1, device_id={"geo": geo - 1}, device_id_type=MESH)
+
+    @pl.when(has_high)
+    def _():
+        pl.semaphore_signal(barrier, inc=1, device_id={"geo": geo + 1}, device_id_type=MESH)
+
+    pl.semaphore_wait(barrier, jnp.minimum(geo, 1) + jnp.minimum(ends - geo, 1))
+
+    def copies(side):
+        at = pl.ds(0, HALO) if side else pl.ds(rows - HALO, HALO)
+        to = {"geo": geo - 1} if side else {"geo": geo + 1}
+        pairs = [
+            (spectrum.at[:, at], near.at[side]),
+            (mask.at[at], near_mask.at[side]),
+            (speed.at[at], near_speed.at[side]),
+            (angle.at[at], near_angle.at[side]),
+        ]
+        return [
+            pltpu.make_async_remote_copy(
+                src_ref=src, dst_ref=dst, send_sem=send.at[side, k], recv_sem=recv.at[side, k],
+                device_id=to, device_id_type=MESH,
+            )
+            for k, (src, dst) in enumerate(pairs)
+        ]
+
+    down, up = copies(1), copies(0)
+
+    @pl.when(has_low)
+    def _():
+        for c in down:
+            c.start()
+
+    @pl.when(has_high)
+    def _():
+        for c in up:
+            c.start()
+
+    for side, missing in ((0, geo == 0), (1, geo == ends)):
+
+        @pl.when(missing)
+        def _(side=side):
+            for ref in (near, near_mask, near_speed, near_angle):
+                ref[side] = jnp.zeros(ref.shape[1:], ref.dtype)
+
+    @pl.when(has_low)
+    def _():
+        for c in down:
+            c.wait_send()
+        for c in up:
+            c.wait_recv()
+
+    @pl.when(has_high)
+    def _():
+        for c in up:
+            c.wait_send()
+        for c in down:
+            c.wait_recv()
+
+
+def geo_halo(spectrum, mask, speed, angle):
+    comps, _, cols = spectrum.shape
+    flat = lambda a: jax.ShapeDtypeStruct((2, HALO, cols), a.dtype)
+    return pl.pallas_call(
+        geo_halo_kernel,
+        in_specs=[ANY] * 4,
+        out_specs=[WHOLE] * 4,
+        out_shape=[jax.ShapeDtypeStruct((2, comps, HALO, cols), spectrum.dtype), flat(mask), flat(speed), flat(angle)],
+        scratch_shapes=[DMA((2, 4)), DMA((2, 4))],
+        compiler_params=pltpu.CompilerParams(collective_id=1, has_side_effects=True),
+        name="geo_halo",
+    )(spectrum, mask, speed, angle)
+
+
+def directions(comps, periodic):
+    if not periodic:
+        return True, True, True, True
+    cos = [math.cos(2 * math.pi * c / ND) for c in comps]
+    sin = [math.sin(2 * math.pi * c / ND) for c in comps]
+    tiny = 1e-3
+    south = any(s > -tiny and c % ND for s, c in zip(sin, comps))
+    north = any(s < tiny and c % ND for s, c in zip(sin, comps))
+    return any(c > -tiny for c in cos), any(c < tiny for c in cos), south, north
+
+
+def march(cells, mask, coef, groups, ways, low, count, stride):
+    west, east, south, north = ways
+    cols = cells.shape[1]
+    steps = PROP_STEPS
+    lag = 2 if south and north else 1
+    depth = 3 if lag == 2 else 2
+    down = north and not south
+    size = len(groups)
+    factor = [[coef[k, pl.ds(g * 8, 8), :] for k in range(5)] for g in groups]
+    span = count + 2 * steps if lag == 2 else count + steps
+    first = low - steps if lag == 2 or not down else low
+    last = first + span - 1
+    trips = span + lag * steps
+    unroll = 6 if lag == 2 else 4
+    trips = -(-trips // unroll) * unroll
+
+    def place(i):
+        return last - i if down else first + i
+
+    def one(i, state):
+        fresh = []
+        for j, g in enumerate(groups):
+            levels = state[j]
+            c, w, e, s, n = factor[j]
+            made = [cells[pl.ds(pl.multiple_of(place(i) * stride + g * 8, 8), 8), :]]
+            for k in range(1, steps + 1):
+                past = levels[k - 1]
+                here = past[0] if lag == 1 else past[1]
+                v = c * here
+                if west:
+                    v = v + w * pltpu.roll(here, 1, 1)
+                if east:
+                    v = v + e * pltpu.roll(here, cols - 1, 1)
+                if lag == 2:
+                    v = v + s * past[2] + n * past[0]
+                elif south:
+                    v = v + s * past[1]
+                elif north:
+                    v = v + n * past[1]
+                made.append(v * mask[place(i - lag * k)])
+            at = pl.multiple_of(place(i - lag * steps) * stride + g * 8, 8)
+            cells[pl.ds(at, 8), :] = made[steps]
+            fresh.append(tuple((made[k],) + levels[k][:-1] for k in range(steps)))
+        return tuple(fresh)
+
+    zero = jnp.zeros((8, cols), F32)
+    start = tuple(tuple((zero,) * depth for _ in range(steps)) for _ in range(size))
+
+    def several(t, state):
+        for u in range(unroll):
+            state = one(t * unroll + u, state)
+        return state
+
+    lax.fori_loop(0, trips // unroll, several, start)
+
+
+def spread_kernel(periodic, spectrum, near, mask, coef, density, tiles, staged, cells, packed, sems, out_sems):
+    comps, rows, cols = staged.shape
+    stride = stride_of(comps) + 8
+    block = 16
+    blocks = comps // block
+    bands = out_sems.shape[0] - 1
+    band = rows // bands
+
+    def fetch(b):
+        at = pl.ds(b * block, block)
+        return pltpu.make_async_copy(spectrum.at[at], staged.at[at], sems.at[b])
+
+    for b in range(blocks):
+        fetch(b).start()
+
+    def turn(b, carry):
+        fetch(b).wait()
+
+        def one(k, carry):
+            c = b * block + k
+            v = jnp.concatenate([near[0, c].astype(F32), staged[c].astype(F32), near[1, c].astype(F32)], axis=0)
+            cells[pl.ds(PAD * stride + c, rows + 2 * HALO, stride=stride), :] = v
+            return carry
+
+        return lax.fori_loop(0, block, one, carry)
+
+    lax.fori_loop(0, blocks, turn, 0)
+
+    low = PAD + HALO - 1
+    groups = comps // 8
+    half = groups // 2 if groups % 2 == 0 else 0
+    for g in range(half if half else groups):
+        pair = [g, g + half] if half else [g]
+        ways = directions([8 * p + k for p in pair for k in range(8)], periodic)
+        march(cells, mask, coef, pair, ways, low, rows + 2, stride)
+
+    whole = pltpu.make_async_copy(
+        cells.at[pl.ds(low * stride, (rows + 2) * stride)], density, out_sems.at[bands]
+    )
+    whole.start()
+
+    def give(b):
+        at = pl.ds(b * band, band)
+        return pltpu.make_async_copy(packed.at[at], tiles.at[at], out_sems.at[b])
+
+    def pack(b, carry):
+        def one(k, carry):
+            t = b * band + k
+            row = jnp.where(t == 0, 0, jnp.where(t == 1, rows - 1, t - 1))
+            at = pl.multiple_of((PAD + HALO + row) * stride, 8)
+            packed[t] = cells[pl.ds(at, comps), :].astype(BF16)
+            return carry
+
+        lax.fori_loop(0, band, one, 0)
+        give(b).start()
+        return carry
+
+    lax.fori_loop(0, bands, pack, 0)
+
+    def drain(b, carry):
+        give(b).wait()
+        return carry
+
+    lax.fori_loop(0, bands, drain, 0)
+    whole.wait()
+
+
+def spread(spectrum, near, mask, coef, periodic):
+    comps, rows, cols = spectrum.shape
+    stride = stride_of(comps) + 8
+    bands = 8 if rows % 8 == 0 else 1
+    return pl.pallas_call(
+        functools.partial(spread_kernel, periodic),
+        in_specs=[ANY, WHOLE, WHOLE, WHOLE],
+        out_specs=[ANY, ANY],
+        out_shape=[
+            jax.ShapeDtypeStruct(((rows + 2) * stride, cols), F32),
+            jax.ShapeDtypeStruct((rows, comps, cols), BF16),
+        ],
+        scratch_shapes=[
+            VMEM((comps, rows, cols), BF16),
+            VMEM(((rows + 2 * HALO + 2 * PAD) * stride, cols), F32),
+            VMEM((rows, comps, cols), BF16),
+            DMA((comps // 16,)),
+            DMA((bands + 1,)),
+        ],
+        compiler_params=pltpu.CompilerParams(vmem_limit_bytes=48 * 1024 * 1024),
+        name="spread",
+    )(spectrum, near, mask, coef)
+
+
+def partner(me, k, peers):
+    if peers & (peers - 1):
+        return lax.rem(me + k, peers)
+    other, bit = me, 1
+    while bit < peers:
+        if k & bit:
+            other = other + bit - 2 * bit * lax.rem(lax.div(other, bit), 2)
+        bit *= 2
+    return other
+
+
+def exchange_kernel(
+    order, tiles, loss, first_in, second_in, merge_in, back, edge,
+    spectra, incs, first, second, merge, product,
+    weight_sems, send_sem, recv_sem, return_sem, back_sem, edge_send, edge_recv,
+):
+    peers = lax.axis_size("comp")
+    me = lax.axis_index("comp")
+    geo, ends = lax.axis_index("geo"), lax.axis_size("geo") - 1
+    chunks, width, comps, cols = spectra.shape
+    local = comps // peers
+    terms = product.shape[0]
+    has_low, has_high = geo > 0, geo < ends
+
+    barrier = pltpu.get_barrier_semaphore()
+    for k in range(1, peers):
+        pl.semaphore_signal(barrier, inc=1, device_id={"comp": partner(me, k, peers)}, device_id_type=MESH)
+
+    @pl.when(has_low)
+    def _():
+        pl.semaphore_signal(barrier, inc=1, device_id={"geo": geo - 1}, device_id_type=MESH)
+
+    @pl.when(has_high)
+    def _():
+        pl.semaphore_signal(barrier, inc=1, device_id={"geo": geo + 1}, device_id_type=MESH)
+
+    pl.semaphore_wait(barrier, peers - 1 + jnp.minimum(geo, 1) + jnp.minimum(ends - geo, 1))
+
+    def part(who):
+        return pl.ds(pl.multiple_of(who * local, 16), local)
+
+    def outward(c, who):
+        return pltpu.make_async_remote_copy(
+            src_ref=tiles.at[pl.ds(c * width, width), who],
+            dst_ref=spectra.at[c, :, part(me)],
+            send_sem=send_sem, recv_sem=recv_sem.at[c],
+            device_id={"comp": who}, device_id_type=MESH,
+        )
+
+    def homeward(c, who):
+        return pltpu.make_async_remote_copy(
+            src_ref=incs.at[c, :, part(who)],
+            dst_ref=back.at[pl.ds(c * width, width), me],
+            send_sem=return_sem, recv_sem=back_sem.at[c],
+            device_id={"comp": who}, device_id_type=MESH,
+        )
+
+    def own_out(c):
+        return pltpu.make_async_copy(tiles.at[pl.ds(c * width, width), me], spectra.at[c, :, part(me)], recv_sem.at[c])
+
+    def own_home(c):
+        return pltpu.make_async_copy(incs.at[c, :, part(me)], back.at[pl.ds(c * width, width), me], back_sem.at[c])
+
+    for group in order:
+
+        def launch(c, carry, group=group):
+            for k in group:
+                outward(c, partner(me, k, peers)).start()
+            return carry
+
+        lax.fori_loop(0, chunks, launch, 0)
+
+    def launch_own(c, carry):
+        own_out(c).start()
+        return carry
+
+    lax.fori_loop(0, chunks, launch_own, 0)
+    loads = [
+        pltpu.make_async_copy(src, dst, weight_sems.at[k])
+        for k, (src, dst) in enumerate(((first_in, first), (second_in, second), (merge_in, merge)))
+    ]
+    for load in loads:
+        load.start()
+    for load in loads:
+        load.wait()
+
+    tile = max(t for t in range(16, 600, 16) if terms % t == 0)
+    step = max(g for g in range(1, peers + 1) if peers % g == 0 and g * local <= 600) * local
+
+    def work(c, carry):
+        pltpu.make_async_copy(spectra.at[c], spectra.at[c], recv_sem.at[c]).wait()
+
+        def both():
+            return jnp.concatenate([spectra[c, h] for h in range(width)], axis=1)
+
+        def multiply(t, carry):
+            rows = pl.ds(pl.multiple_of(t * tile, 16), tile)
+            x = both()
+            one = jnp.dot(first[rows, :], x, preferred_element_type=F32)
+            two = jnp.dot(second[rows, :], x, preferred_element_type=F32)
+            product[rows, :] = (one * two).astype(BF16)
+            return carry
+
+        lax.fori_loop(0, terms // tile, multiply, 0)
+        roots = []
+        for h in range(width):
+            energy = jnp.sum(spectra[c, h].astype(F32), axis=0, keepdims=True)
+            roots.append(jnp.sqrt(energy / comps + 1e-06))
+        for d in range(0, comps, step):
+            rows = slice(d, d + step)
+            moved = jnp.dot(merge[rows, :], product[...], preferred_element_type=F32)
+            for h in range(width):
+                lanes = slice(h * cols, (h + 1) * cols)
+                total = moved[:, lanes] - loss[rows, :] * roots[h] * spectra[c, h, rows, :].astype(F32)
+                incs[c, h, rows, :] = total.astype(BF16)
+        for group in order:
+            for k in group:
+                homeward(c, partner(me, k, peers)).start()
+        own_home(c).start()
+        return carry
+
+    lax.fori_loop(0, chunks, work, 0)
+
+    def landed(c):
+        there = back.at[pl.ds(c * width, width)]
+        pltpu.make_async_copy(there, there, back_sem.at[c]).wait()
+
+    landed(0)
+    to_low = pltpu.make_async_remote_copy(
+        src_ref=back.at[0, 0], dst_ref=edge.at[1], send_sem=edge_send.at[1], recv_sem=edge_recv.at[1],
+        device_id={"geo": geo - 1}, device_id_type=MESH,
+    )
+    to_high = pltpu.make_async_remote_copy(
+        src_ref=back.at[0, 1], dst_ref=edge.at[0], send_sem=edge_send.at[0], recv_sem=edge_recv.at[0],
+        device_id={"geo": geo + 1}, device_id_type=MESH,
+    )
+
+    @pl.when(has_low)
+    def _():
+        to_low.start()
+
+    @pl.when(has_high)
+    def _():
+        to_high.start()
+
+    def rest(c, carry):
+        landed(c)
+        return carry
+
+    lax.fori_loop(1, chunks, rest, 0)
+
+    @pl.when(has_low)
+    def _():
+        to_low.wait_send()
+        to_high.wait_recv()
+
+    @pl.when(has_high)
+    def _():
+        to_high.wait_send()
+        to_low.wait_recv()
+
+    def sent(c, carry):
+        for k in range(1, peers):
+            outward(c, partner(me, k, peers)).wait_send()
+            homeward(c, partner(me, k, peers)).wait_send()
+        return carry
+
+    lax.fori_loop(0, chunks, sent, 0)
+
+
+def exchange(tiles, loss, first, second, merge):
+    rows, local, cols = tiles.shape
+    peers = lax.axis_size("comp")
+    depth = rows // peers
+    chunks = depth // CHUNK
+    comps, terms = merge.shape
+    tiles = tiles.reshape(depth, peers, local, cols)
+    if peers == 8:
+        order = [(1, 2, 3), (4, 5, 6, 7)]
+    else:
+        order = [tuple(range(1, peers))]
+    return pl.pallas_call(
+        functools.partial(exchange_kernel, order),
+        in_specs=[ANY, WHOLE, ANY, ANY, ANY],
+        out_specs=[ANY, ANY],
+        out_shape=[
+            jax.ShapeDtypeStruct((depth, peers, local, cols), BF16),
+            jax.ShapeDtypeStruct((2, local, cols), BF16),
+        ],
+        scratch_shapes=[
+            VMEM((chunks, CHUNK, comps, cols), BF16),
+            VMEM((chunks, CHUNK, comps, cols), BF16),
+            VMEM((terms, comps), BF16),
+            VMEM((terms, comps), BF16),
+            VMEM((comps, terms), BF16),
+            VMEM((terms, CHUNK * cols), BF16),
+            DMA((3,)),
+            DMA,
+            DMA((chunks,)),
+            DMA,
+            DMA((chunks,)),
+            DMA((2,)),
+            DMA((2,)),
+        ],
+        cost_estimate=pl.CostEstimate(
+            flops=6 * comps * terms * depth * cols, bytes_accessed=6 * comps * terms, transcendentals=0
+        ),
+        compiler_params=pltpu.CompilerParams(
+            collective_id=2, has_side_effects=True, vmem_limit_bytes=60 * 1024 * 1024
+        ),
+        name="exchange",
+    )(tiles, loss, first, second, merge)
+
+
+def close_kernel(periodic, ends, density, back, edge, wind, mask, coef, out, cells, incs, staged, sems, out_sems):
+    comps, rows, cols = staged.shape
+    stride = cells.shape[0] // (rows + 2)
+    block = 16
+    blocks = comps // block
+    turned = cells.reshape(rows + 2, stride, cols)
+    source = density.reshape(rows + 2, stride, cols)
+
+    def fetches(b):
+        at = pl.ds(pl.multiple_of(b * block, block), block)
+        moves = [
+            (source.at[:, at], turned.at[:, at]),
+            (edge.at[0, at], incs.at[0, at]),
+            (back.at[0, at], incs.at[1, at]),
+            (back.at[pl.ds(2, rows - 2), at], incs.at[pl.ds(2, rows - 2), at]),
+            (back.at[1, at], incs.at[rows, at]),
+            (edge.at[1, at], incs.at[rows + 1, at]),
+        ]
+        return [pltpu.make_async_copy(src, dst, sems.at[b, k]) for k, (src, dst) in enumerate(moves)]
+
+    def give(b):
+        at = pl.ds(b * block, block)
+        return pltpu.make_async_copy(staged.at[at], out.at[at], out_sems.at[b])
+
+    for b in range(blocks):
+        for f in fetches(b):
+            f.start()
+
+    for b in range(blocks):
+        for f in fetches(b):
+            f.wait()
+        span = slice(b * block, (b + 1) * block)
+        for side, at in ((0, 0), (1, rows + 1)):
+
+            @pl.when(ends[side] == 1)
+            def _(at=at, span=span):
+                incs[at, span, :] = jnp.zeros((block, cols), BF16)
+
+        pair = [2 * b, 2 * b + 1]
+        ways = [directions([8 * g + k for k in range(8)], periodic) for g in pair]
+        factor = [[coef[k, pl.ds(g * 8, 8), :] for k in range(8)] for g in pair]
+
+        def one(i, state):
+            both = incs[i, span, :].astype(F32)
+            blow, turn_x, turn_y = wind[0, i], wind[1, i], wind[2, i]
+            sea = mask[i - 1]
+            fresh = []
+            for j, g in enumerate(pair):
+                c, w, e, s, n, rate, cos_h, sin_h = factor[j]
+                west, east, south, north = ways[j]
+                here, past = state[j]
+                at = pl.multiple_of(i * stride + g * 8, 8)
+                d = cells[pl.ds(at, 8), :]
+                facing = jnp.maximum(cos_h * turn_x + sin_h * turn_y, 0.0)
+                growth = rate * blow * (facing * facing)
+                new = d + growth * d + both[j * 8 : (j + 1) * 8]
+                v = c * here
+                if west:
+                    v = v + w * pltpu.roll(here, 1, 1)
+                if east:
+                    v = v + e * pltpu.roll(here, cols - 1, 1)
+                if south:
+                    v = v + s * past
+                if north:
+                    v = v + n * new
+                back_at = pl.multiple_of((i - 1) * stride + g * 8, 8)
+                cells[pl.ds(back_at, 8), :] = v * sea
+                fresh.append((new, here))
+            return tuple(fresh)
+
+        def first(i):
+            both = incs[i, span, :].astype(F32)
+            made = []
+            for j, g in enumerate(pair):
+                rate, cos_h, sin_h = factor[j][5:8]
+                d = cells[pl.ds(i * stride + g * 8, 8), :]
+                facing = jnp.maximum(cos_h * wind[1, i] + sin_h * wind[2, i], 0.0)
+                growth = rate * wind[0, i] * (facing * facing)
+                made.append((d + growth * d + both[j * 8 : (j + 1) * 8], jnp.zeros((8, cols), F32)))
+            return tuple(made)
+
+        def two(t, state):
+            return one(2 * t + 2, one(2 * t + 1, state))
+
+        state = lax.fori_loop(0, (rows + 1) // 2, two, first(0))
+        if (rows + 1) % 2:
+            one(rows + 1, state)
+
+    def finish_block(b, carry):
+        def lift(k, carry):
+            c = b * block + k
+            staged[c] = cells[pl.ds(stride + c, rows, stride=stride), :].astype(BF16)
+            return carry
+
+        lax.fori_loop(0, block, lift, 0)
+        give(b).start()
+        return carry
+
+    lax.fori_loop(0, blocks, finish_block, 0)
+
+    def drain(b, carry):
+        give(b).wait()
+        return carry
+
+    lax.fori_loop(0, blocks, drain, 0)
+
+
+def close(density, back, edge, wind, mask, coef, ends, periodic):
+    rows, comps, cols = back.shape
+    stride = stride_of(comps) + 8
+    return pl.pallas_call(
+        functools.partial(close_kernel, periodic),
+        in_specs=[pl.BlockSpec(memory_space=SMEM), ANY, ANY, ANY, WHOLE, WHOLE, WHOLE],
+        out_specs=ANY,
+        out_shape=jax.ShapeDtypeStruct((comps, rows, cols), BF16),
+        scratch_shapes=[
+            VMEM(((rows + 2) * stride, cols), F32),
+            VMEM((rows + 2, comps, cols), BF16),
+            VMEM((comps, rows, cols), BF16),
+            DMA((comps // 16, 6)),
+            DMA((comps // 16,)),
+        ],
+        compiler_params=pltpu.CompilerParams(vmem_limit_bytes=48 * 1024 * 1024),
+        name="close",
+    )(ends, density, back, edge, wind, mask, coef)
+
+
+def tall(rows_of, lead):
+    rows_of = jnp.pad(rows_of, ((lead, lead), (0, 0)))
+    return jnp.broadcast_to(rows_of[:, None, :], (rows_of.shape[0], 8, rows_of.shape[1]))
+
+
+def body(spectrum, land_mask, wind_speed, wind_dir, input_rate, dissipation, pair_first, pair_second, merge_weight):
+    local, rows, cols = spectrum.shape
+    peers = lax.axis_size("comp")
+    fits = local % 16 == 0 and rows % (peers * CHUNK) == 0 and rows % 16 == 0 and cols == 128
+    if not fits:
+        return plain_body(
+            spectrum, land_mask, wind_speed, wind_dir, input_rate, dissipation, pair_first, pair_second, merge_weight
+        )
+    periodic = local % ND == 0
+    near, near_mask, near_speed, near_angle = geo_halo(spectrum, land_mask, wind_speed, wind_dir)
+
+    ids = lax.axis_index("comp") * local + jnp.arange(local, dtype=jnp.int32)
+    frequency = (ids // ND).astype(F32)
+    heading = 2.0 * math.pi * (ids % ND).astype(F32) / ND
+    courant = 0.7 * jnp.power(F32(1.1), -frequency)
+    cos_h, sin_h = jnp.cos(heading), jnp.sin(heading)
+    west, east = jnp.maximum(courant * cos_h, 0.0), jnp.maximum(-courant * cos_h, 0.0)
+    south, north = jnp.maximum(courant * sin_h, 0.0), jnp.maximum(-courant * sin_h, 0.0)
+    center = 1.0 - west - east - south - north
+    coef = jnp.stack([center, west, east, south, north, input_rate, cos_h, sin_h])
+    coef = jnp.broadcast_to(coef[:, :, None], (8, local, cols))
+
+    sea = jnp.concatenate([near_mask[0], land_mask, near_mask[1]]).astype(F32)
+    sea = tall(sea, PAD)
+    angle = jnp.concatenate([near_angle[0, HALO - 1 :], wind_dir, near_angle[1, :1]])
+    speed = jnp.concatenate([near_speed[0, HALO - 1 :], wind_speed, near_speed[1, :1]])
+    wind = jnp.stack([tall(speed, 0), tall(jnp.cos(angle), 0), tall(jnp.sin(angle), 0)])
+    geo = lax.axis_index("geo")
+    ends = jnp.stack([geo == 0, geo == lax.axis_size("geo") - 1]).astype(jnp.int32)
+
+    density, tiles = spread(spectrum, near, sea, coef, periodic)
+    back, edge = exchange(tiles, dissipation[:, None], pair_first, pair_second, merge_weight)
+    below = PAD + HALO - 1
+    return close(density, back.reshape(rows, local, cols), edge, wind, sea[below : below + rows + 2], coef, ends, periodic)
+
+
 def solution(mesh):
     placed = (P("comp", "geo", None), P("geo", None), P("geo", None), P("geo", None), P("comp"), P(), P(), P(), P())
     return jax.shard_map(

time: 345 us -> 380 us (1.10)
  Pallas kernels: 165 us -> 367 us
  waiting for transfers between devices: 110 us -> 0 us
  starting transfers between devices: 35.2 us -> 0 us
  other arithmetic: 12.3 us -> 0.74 us
  local copies, waits for them, and re-layouts: 21 us -> 10.4 us
    pallas_call x6 -> x4, Pallas kernels: 165 us -> 367 us  [the longest x1 209 us: exchange(): pl.pallas_call(functools.partial(exchange_kernel, order), in_specs=[ANY,...]
    all_to_all x5 -> x0, waiting for transfers between devices: 109 us -> none  [the longest x2 68.7 us: body(): lax.all_to_all(inc, 'comp', split_axis=0, concat_axis=0, tiled=True)]
    all_to_all x5 -> x0, starting transfers between devices: 21.9 us -> none  [the longest x3 14 us: body(): lax.all_to_all(out, 'comp', split_axis=0, concat_axis=0, tiled=True)]
    ppermute x6 -> x0, starting transfers between devices: 13.3 us -> none  [the longest x2 8.15 us: edges(): lower = lax.ppermute(tail, 'geo', [(i, i + 1) for i in range(ends)])]
    concatenate x2 -> x1, other arithmetic: 9.72 us -> 0.01 us  [body(): jnp.concatenate([near_speed[0, HALO - 1:], wind_speed, near_speed[1, :1]])]
    slice x11 -> x1, local copies, waits for them, and re-layouts: 9.69 us -> 0.01 us  [body(): sea[below:below + rows + 2]]
  transfers between devices with their start and end apart: 11 -> 0, of which waited for: 6 -> 0; matrix products, arithmetic and copies ran while one was open for 9% -> 0% of each run, Pallas kernels for 25% -> 0%
where the time goes in v1:
time: 380 us; the launch traced here: 378 us
  Pallas kernels  367 us (97%)
  local copies, waits for them, and re-layouts  10.4 us (3%)
    pallas_call x1, Pallas kernels, exchange(): pl.pallas_call(functools.partial(exchange_kernel, order), in_specs=[ANY,...  209 us
    pallas_call x1, Pallas kernels, spread(): pl.pallas_call(functools.partial(spread_kernel, periodic), in_specs=[ANY,...  96.4 us
    pallas_call x1, Pallas kernels, close(): pl.pallas_call(functools.partial(close_kernel, periodic), in_specs=[pl.Bl...  56.1 us

profile of v1, /device:TPU:0, one launch (start us, length us, event | category | flops | bytes accessed | tf_op | source)
XLA Modules:
  0.0 378.4 jit_solution(7300111565783501921)
XLA Ops:
  0.0 0.0 copy-start.3
  0.0 0.0 copy-start.6
  0.0 0.1 add_convert_fusion.1.ends
  0.1 5.3 %geo_halo.1 = (bf16[2,144,8,128]{3,2,1,0:T(8,128)(2,1)}, s32[2,8,128]{2,1,0:T(8,128)}, f32[2,8,128]{2,1,0:T(8,128)}, f32[2,8,128]{2,1,0:T(8,128)}) custom-call(bf16[144,128,128]{2,1,0:T(8,128)(2,1)} %spectrum.3, s32[128,128]{1,0:T(8,128)} %mask.1, f32[128,128]{1,0:T(8,128)} %speed.1, f32[128,128]{1,0:T(8,128)} %angle.1), custom_call_target="tpu_custom_call" | custom-call | tf_op jit(solution)/shard_map/geo_halo/pallas_call | solution.py:367
  5.4 0.7 slice_bitcast_fusion.1
  6.1 0.0 copy-done.3
  6.2 0.0 copy-start.5
  6.2 0.1 multiply_maximum_fusion
  6.3 0.1 multiply_maximum_fusion.3
  6.4 0.1 multiply_maximum_fusion.1
  6.4 0.1 fusion.6
  6.5 0.0 copy-done.6
  6.6 0.2 broadcast_in_dim.9.coef
  6.8 0.0 copy-start
  6.8 1.1 copy-done
  7.8 96.4 %spread.1 = (f32[19760,128]{1,0:T(8,128)}, bf16[128,144,128]{2,1,0:T(8,128)(2,1)}) custom-call(bf16[144,128,128]{2,1,0:T(8,128)(2,1)} %spectrum.3, bf16[2,144,8,128]{3,2,1,0:T(8,128)(2,1)S(1)} %copy-done, f32[176,8,128]{2,1,0:T(8,128)S(1)} %broadcast_in_dim.8.mask, f32[8,144,128]{2,1,0:T(8,128)S(1)} %broadcast_in_dim.9.coef), custom_call_target="tpu_custom_call" | custom-call | tf_op jit(solution)/shard_map/spread/pallas_call | solution.py:516
  104.3 0.0 copy-done.5
  104.3 1.0 broadcast_in_dim.24.loss
  105.3 6.4 %copy.12.merge_in = bf16[1152,1728]{1,0:T(8,128)(2,1)} copy(bf16[1152,1728]{0,1:T(8,128)(2,1)} %param.17) | data formatting | bytes 7962624 | tf_op args[8]
  111.7 0.0 copy-start.2
  111.7 0.0 copy-start.4
  111.7 209.3 %exchange.1 = (bf16[16,8,144,128]{3,2,1,0:T(8,128)(2,1)}, bf16[2,144,128]{2,1,0:T(8,128)(2,1)}) custom-call(bf16[16,8,144,128]{3,2,1,0:T(8,128)(2,1)} %bitcast.19, f32[1152,1]{1,0:T(8,128)} %broadcast_in_dim.24.loss, bf16[1728,1152]{1,0:T(8,128)(2,1)} %first_in.1, bf16[1728,1152]{1,0:T(8,128)(2,1)} %second_in.1, bf16[1152,1728]{1,0:T(8,128)(2,1)} %copy.12.merge_in), custom_call_target="tpu_custom_call" | custom-call | flops 24461180928 | bytes 11943936 | tf_op jit(solution)/shard_map/exchange/pallas_call | solution.py:717
  321.0 0.0 copy-start.1
  321.0 0.7 slice_bitcast_fusion.3
  321.7 0.0 copy-done.2
  321.7 0.3 fusion.1
  322.1 0.0 copy-done.4
  322.2 0.1 pad_maximum_fusion.wind
  322.3 0.0 copy-done.1
  322.3 56.1 %close.1 = bf16[144,128,128]{2,1,0:T(8,128)(2,1)} custom-call(s32[2]{0:T(128)S(1)} %add_convert_fusion.1.ends, f32[19760,128]{1,0:T(8,128)} %get-tuple-element.15.density, bf16[128,144,128]{2,1,0:T(8,128)(2,1)} %bitcast.17, bf16[2,144,128]{2,1,0:T(8,128)(2,1)S(1)} %copy-done.1, f32[3,130,8,128]{3,2,1,0:T(8,128)S(1)} %pad_maximum_fusion.wind, ...), custom_call_target="tpu_custom_call" | custom-call | tf_op jit(solution)/shard_map/close/pallas_call | solution.py:860
  (10 shorter events, 0.3 us)
Async XLA Ops:
  0.0 6.1 %copy-start.3 = (s32[128,128]{1,0:T(8,128)S(1)}, s32[128,128]{1,0:T(8,128)}, u32[]{:S(2)}) copy-start(s32[128,128]{1,0:T(8,128)} %mask.1) | copy-start | bytes 196612
  0.0 6.5 %copy-start.6 = (f32[144]{0:T(256)S(1)}, f32[144]{0:T(256)}, u32[]{:S(2)}) copy-start(f32[144]{0:T(256)} %param.13) | copy-start | bytes 1732
  6.2 98.1 %copy-start.5 = (f32[1152]{0:T(1024)S(1)}, f32[1152]{0:T(1024)}, u32[]{:S(2)}) copy-start(f32[1152]{0:T(1024)} %param.14) | copy-start | bytes 13828
  6.8 1.1 copy-start
  111.7 210.0 %copy-start.2 = (f32[128,128]{1,0:T(8,128)S(1)}, f32[128,128]{1,0:T(8,128)}, u32[]{:S(2)}) copy-start(f32[128,128]{1,0:T(8,128)} %angle.1) | copy-start | bytes 196612
  111.7 210.4 %copy-start.4 = (f32[128,128]{1,0:T(8,128)S(1)}, f32[128,128]{1,0:T(8,128)}, u32[]{:S(2)}) copy-start(f32[128,128]{1,0:T(8,128)} %speed.1) | copy-start | bytes 196612
  321.0 1.3 copy-start.1

commit v2 on v1

--- a/solution.py
+++ b/solution.py
@@ -20,8 +20,10 @@
 WHOLE = pl.BlockSpec(memory_space=pltpu.VMEM)
 MESH = pl.DeviceIdType.MESH
 DMA = pltpu.SemaphoreType.DMA
-PAD = 16
 CHUNK = 2
+BAND = 32
+RUN = 12
+SPAN = BAND + 2 * HALO
 SMEM = pltpu.SMEM
 
 
@@ -386,151 +388,122 @@
     return any(c > -tiny for c in cos), any(c < tiny for c in cos), south, north
 
 
-def march(cells, mask, coef, groups, ways, low, count, stride):
-    west, east, south, north = ways
-    cols = cells.shape[1]
-    steps = PROP_STEPS
-    lag = 2 if south and north else 1
-    depth = 3 if lag == 2 else 2
-    down = north and not south
-    size = len(groups)
-    factor = [[coef[k, pl.ds(g * 8, 8), :] for k in range(5)] for g in groups]
-    span = count + 2 * steps if lag == 2 else count + steps
-    first = low - steps if lag == 2 or not down else low
-    last = first + span - 1
-    trips = span + lag * steps
-    unroll = 6 if lag == 2 else 4
-    trips = -(-trips // unroll) * unroll
-
-    def place(i):
-        return last - i if down else first + i
-
-    def one(i, state):
-        fresh = []
-        for j, g in enumerate(groups):
-            levels = state[j]
-            c, w, e, s, n = factor[j]
-            made = [cells[pl.ds(pl.multiple_of(place(i) * stride + g * 8, 8), 8), :]]
-            for k in range(1, steps + 1):
-                past = levels[k - 1]
-                here = past[0] if lag == 1 else past[1]
-                v = c * here
-                if west:
-                    v = v + w * pltpu.roll(here, 1, 1)
-                if east:
-                    v = v + e * pltpu.roll(here, cols - 1, 1)
-                if lag == 2:
-                    v = v + s * past[2] + n * past[0]
-                elif south:
-                    v = v + s * past[1]
-                elif north:
-                    v = v + n * past[1]
-                made.append(v * mask[place(i - lag * k)])
-            at = pl.multiple_of(place(i - lag * steps) * stride + g * 8, 8)
-            cells[pl.ds(at, 8), :] = made[steps]
-            fresh.append(tuple((made[k],) + levels[k][:-1] for k in range(steps)))
-        return tuple(fresh)
-
-    zero = jnp.zeros((8, cols), F32)
-    start = tuple(tuple((zero,) * depth for _ in range(steps)) for _ in range(size))
-
-    def several(t, state):
-        for u in range(unroll):
-            state = one(t * unroll + u, state)
-        return state
-
-    lax.fori_loop(0, trips // unroll, several, start)
-
-
-def spread_kernel(periodic, spectrum, near, mask, coef, density, tiles, staged, cells, packed, sems, out_sems):
-    comps, rows, cols = staged.shape
-    stride = stride_of(comps) + 8
-    block = 16
+def column_terms(x, w, e, west, east):
+    cols = x.shape[1]
+    if west and east:
+        return w * pltpu.roll(x, 1, 1) + e * pltpu.roll(x, cols - 1, 1)
+    return w * pltpu.roll(x, 1, 1) if west else e * pltpu.roll(x, cols - 1, 1)
+
+
+def group_sets(comps, periodic):
+    groups = comps // 8
+    count = max(k for k in range(1, 7) if groups % k == 0)
+    sets = [list(range(k * count, (k + 1) * count)) for k in range(groups // count)]
+    ways = [directions([8 * g + k for k in range(8)], periodic) for g in range(groups)]
+    return sets, ways
+
+
+def substeps(field, work, done, mask, coef, side, group_set, ways, top, base_of, done_at, stride):
+    factor = {g: [coef[k, pl.ds(g * 8, 8), :] for k in range(5)] for g in group_set}
+    size = len(group_set)
+    plans = []
+    for p in range(PROP_STEPS):
+        trim = RUN // 2 if p >= PROP_STEPS - 2 else 0
+        source = (field, base_of) if p == 0 else (work[(p - 1) % 2], 1)
+        target = (done, done_at - trim) if p == PROP_STEPS - 1 else (work[p % 2], 1)
+        plans.append((source, target, trim, (SPAN - 2 * trim) // RUN))
+
+    def at(base, row, g):
+        return pl.ds(pl.multiple_of((base + row) * stride + g * 8, 8), 8)
+
+    def ahead(source, row):
+        ref, base = source
+        made = []
+        for r in range(RUN):
+            for g in group_set:
+                west, east = ways[g][:2]
+                made.append(column_terms(ref[at(base, row + r, g), :], factor[g][1], factor[g][2], west, east))
+        return made
+
+    def keep(made):
+        for k, v in enumerate(made):
+            side[k] = v
+
+    def finish(source, target, row):
+        ref, base = source
+        out, out_base = target
+        for j, g in enumerate(group_set):
+            c, _, _, s, n = factor[g]
+            south, north = ways[g][2:]
+            held = ref[at(base, row - 1, g), :] if south else None
+            here = ref[at(base, row, g), :]
+            for r in range(RUN):
+                after = ref[at(base, row + r + 1, g), :] if north or r < RUN - 1 else None
+                v = c * here + side[r * size + j]
+                if south:
+                    v = v + s * held
+                if north:
+                    v = v + n * after
+                out[at(out_base, row + r, g), :] = v * mask[top + row + r]
+                held, here = here, after
+
+    keep(ahead(plans[0][0], plans[0][2]))
+    for p, (source, target, trim, trips) in enumerate(plans):
+
+        def trip(t, carry, source=source, target=target, trim=trim):
+            row = trim + t * RUN
+            made = ahead(source, row + RUN)
+            finish(source, target, row)
+            keep(made)
+            return carry
+
+        lax.fori_loop(0, trips - 1, trip, 0)
+        row = trim + (trips - 1) * RUN
+        made = ahead(plans[p + 1][0], plans[p + 1][2]) if p + 1 < PROP_STEPS else None
+        finish(source, target, row)
+        if made is not None:
+            keep(made)
+
+
+def turn_in(spectrum, near, staged, field, sems, stride):
+    comps, rows, cols = spectrum.shape
+    slots, block = staged.shape[:2]
     blocks = comps // block
-    bands = out_sems.shape[0] - 1
-    band = rows // bands
+    for at in (0, (rows + 2 * HALO + 1) * stride):
+        field[pl.ds(at, stride), :] = jnp.zeros((stride, cols), F32)
 
     def fetch(b):
-        at = pl.ds(b * block, block)
-        return pltpu.make_async_copy(spectrum.at[at], staged.at[at], sems.at[b])
-
-    for b in range(blocks):
+        slot = lax.rem(b, slots)
+        return pltpu.make_async_copy(spectrum.at[pl.ds(b * block, block)], staged.at[slot], sems.at[slot])
+
+    for b in range(min(slots, blocks)):
         fetch(b).start()
 
     def turn(b, carry):
         fetch(b).wait()
+        slot = lax.rem(b, slots)
 
         def one(k, carry):
             c = b * block + k
-            v = jnp.concatenate([near[0, c].astype(F32), staged[c].astype(F32), near[1, c].astype(F32)], axis=0)
-            cells[pl.ds(PAD * stride + c, rows + 2 * HALO, stride=stride), :] = v
+            v = jnp.concatenate(
+                [near[0, c].astype(F32), staged[slot, k].astype(F32), near[1, c].astype(F32)], axis=0
+            )
+            field[pl.ds(stride + c, rows + 2 * HALO, stride=stride), :] = v
             return carry
 
-        return lax.fori_loop(0, block, one, carry)
+        lax.fori_loop(0, block, one, 0)
+
+        @pl.when(b + slots < blocks)
+        def _():
+            fetch(b + slots).start()
+
+        return carry
 
     lax.fori_loop(0, blocks, turn, 0)
 
-    low = PAD + HALO - 1
-    groups = comps // 8
-    half = groups // 2 if groups % 2 == 0 else 0
-    for g in range(half if half else groups):
-        pair = [g, g + half] if half else [g]
-        ways = directions([8 * p + k for p in pair for k in range(8)], periodic)
-        march(cells, mask, coef, pair, ways, low, rows + 2, stride)
-
-    whole = pltpu.make_async_copy(
-        cells.at[pl.ds(low * stride, (rows + 2) * stride)], density, out_sems.at[bands]
-    )
-    whole.start()
-
-    def give(b):
-        at = pl.ds(b * band, band)
-        return pltpu.make_async_copy(packed.at[at], tiles.at[at], out_sems.at[b])
-
-    def pack(b, carry):
-        def one(k, carry):
-            t = b * band + k
-            row = jnp.where(t == 0, 0, jnp.where(t == 1, rows - 1, t - 1))
-            at = pl.multiple_of((PAD + HALO + row) * stride, 8)
-            packed[t] = cells[pl.ds(at, comps), :].astype(BF16)
-            return carry
-
-        lax.fori_loop(0, band, one, 0)
-        give(b).start()
-        return carry
-
-    lax.fori_loop(0, bands, pack, 0)
-
-    def drain(b, carry):
-        give(b).wait()
-        return carry
-
-    lax.fori_loop(0, bands, drain, 0)
-    whole.wait()
-
-
-def spread(spectrum, near, mask, coef, periodic):
-    comps, rows, cols = spectrum.shape
-    stride = stride_of(comps) + 8
-    bands = 8 if rows % 8 == 0 else 1
-    return pl.pallas_call(
-        functools.partial(spread_kernel, periodic),
-        in_specs=[ANY, WHOLE, WHOLE, WHOLE],
-        out_specs=[ANY, ANY],
-        out_shape=[
-            jax.ShapeDtypeStruct(((rows + 2) * stride, cols), F32),
-            jax.ShapeDtypeStruct((rows, comps, cols), BF16),
-        ],
-        scratch_shapes=[
-            VMEM((comps, rows, cols), BF16),
-            VMEM(((rows + 2 * HALO + 2 * PAD) * stride, cols), F32),
-            VMEM((rows, comps, cols), BF16),
-            DMA((comps // 16,)),
-            DMA((bands + 1,)),
-        ],
-        compiler_params=pltpu.CompilerParams(vmem_limit_bytes=48 * 1024 * 1024),
-        name="spread",
-    )(spectrum, near, mask, coef)
+
+def band_at(k, bands):
+    return jnp.where(k == 0, 0, jnp.where(k == 1, bands - 1, k - 1))
 
 
 def partner(me, k, peers):
@@ -544,9 +517,11 @@
     return other
 
 
-def exchange_kernel(
-    order, tiles, loss, first_in, second_in, merge_in, back, edge,
+def advance_kernel(
+    order, periodic, spectrum, near, mask, coef, loss, first_in, second_in, merge_in, density, back, edge,
+    staged, field, work_a, work_b, done, side, tiles,
     spectra, incs, first, second, merge, product,
+    stage_sems, density_sems, end_sems,
     weight_sems, send_sem, recv_sem, return_sem, back_sem, edge_send, edge_recv,
 ):
     peers = lax.axis_size("comp")
@@ -590,32 +565,94 @@
             device_id={"comp": who}, device_id_type=MESH,
         )
 
-    def own_out(c):
-        return pltpu.make_async_copy(tiles.at[pl.ds(c * width, width), me], spectra.at[c, :, part(me)], recv_sem.at[c])
-
     def own_home(c):
         return pltpu.make_async_copy(incs.at[c, :, part(me)], back.at[pl.ds(c * width, width), me], back_sem.at[c])
 
-    for group in order:
-
-        def launch(c, carry, group=group):
-            for k in group:
-                outward(c, partner(me, k, peers)).start()
-            return carry
-
-        lax.fori_loop(0, chunks, launch, 0)
-
-    def launch_own(c, carry):
-        own_out(c).start()
-        return carry
-
-    lax.fori_loop(0, chunks, launch_own, 0)
     loads = [
         pltpu.make_async_copy(src, dst, weight_sems.at[k])
         for k, (src, dst) in enumerate(((first_in, first), (second_in, second), (merge_in, merge)))
     ]
+    rows = mask.shape[0] - 2 * HALO
+    stride = stride_of(local) + 8
+    bands = rows // BAND
+    turn_in(spectrum, near, staged, field, stage_sems, stride)
     for load in loads:
         load.start()
+    zeros = jnp.zeros((stride, cols), F32)
+    for work in (work_a, work_b):
+        work[pl.ds(0, stride), :] = zeros
+        work[pl.ds((SPAN + 1) * stride, stride), :] = zeros
+
+    sets, ways = group_sets(local, periodic)
+
+    def whole(k):
+        at = lax.rem(k, 2) * (SPAN - RUN)
+        band = band_at(k, bands)
+        return pltpu.make_async_copy(
+            done.at[pl.ds((at + 2) * stride, BAND * stride)],
+            density.at[pl.ds((band * BAND + 1) * stride, BAND * stride)],
+            density_sems.at[k],
+        )
+
+    def end(side_of):
+        k = 1 if side_of and bands > 1 else 0
+        at = (k % 2) * (SPAN - RUN) + (BAND + 2 if side_of else 1)
+        row = rows + 1 if side_of else 0
+        return pltpu.make_async_copy(
+            done.at[pl.ds(at * stride, stride)], density.at[pl.ds(row * stride, stride)], end_sems.at[side_of]
+        )
+
+    def form(k, carry):
+        band = band_at(k, bands)
+        at = lax.rem(k, 2) * (SPAN - RUN)
+
+        @pl.when(k >= 2)
+        def _():
+            whole(k - 2).wait()
+
+        @pl.when(k == 2)
+        def _():
+            end(0).wait()
+
+        if bands > 3:
+
+            @pl.when(k == 3)
+            def _():
+                end(1).wait()
+
+        for group_set in sets:
+            substeps(
+                field, (work_a, work_b), done, mask, coef, side, group_set, ways,
+                band * BAND, band * BAND + 1, at, stride,
+            )
+        whole(k).start()
+
+        @pl.when(k == 0)
+        def _():
+            end(0).start()
+
+        @pl.when(k == min(1, bands - 1))
+        def _():
+            end(1).start()
+
+        def pack(r, carry):
+            t = k * BAND + r
+            from_at = pl.multiple_of((at + 2 + r) * stride, 8)
+            tiles[lax.div(t, peers), lax.rem(t, peers)] = done[pl.ds(from_at, local), :].astype(BF16)
+            return carry
+
+        lax.fori_loop(0, BAND, pack, 0)
+        per = BAND // (peers * width)
+        for group in order:
+            for j in range(per):
+                for who in group:
+                    outward(k * per + j, partner(me, who, peers)).start()
+        for j in range(per):
+            for h in range(width):
+                spectra[k * per + j, h, part(me), :] = tiles[(k * per + j) * width + h, me]
+        return carry
+
+    lax.fori_loop(0, bands, form, 0)
     for load in loads:
         load.wait()
 
@@ -623,7 +660,8 @@
     step = max(g for g in range(1, peers + 1) if peers % g == 0 and g * local <= 600) * local
 
     def work(c, carry):
-        pltpu.make_async_copy(spectra.at[c], spectra.at[c], recv_sem.at[c]).wait()
+        arrived = spectra.at[c, :, pl.ds(0, comps - local)]
+        pltpu.make_async_copy(arrived, arrived, recv_sem.at[c]).wait()
 
         def both():
             return jnp.concatenate([spectra[c, h] for h in range(width)], axis=1)
@@ -660,13 +698,20 @@
         there = back.at[pl.ds(c * width, width)]
         pltpu.make_async_copy(there, there, back_sem.at[c]).wait()
 
-    landed(0)
+    far_chunk = (min(2, bands) * BAND - 1) // (peers * width)
+
+    def land(c, carry):
+        landed(c)
+        return carry
+
+    lax.fori_loop(0, far_chunk + 1, land, 0)
+    last = min(2, bands) * BAND - 1
     to_low = pltpu.make_async_remote_copy(
         src_ref=back.at[0, 0], dst_ref=edge.at[1], send_sem=edge_send.at[1], recv_sem=edge_recv.at[1],
         device_id={"geo": geo - 1}, device_id_type=MESH,
     )
     to_high = pltpu.make_async_remote_copy(
-        src_ref=back.at[0, 1], dst_ref=edge.at[0], send_sem=edge_send.at[0], recv_sem=edge_recv.at[0],
+        src_ref=back.at[last // peers, last % peers], dst_ref=edge.at[0], send_sem=edge_send.at[0], recv_sem=edge_recv.at[0],
         device_id={"geo": geo + 1}, device_id_type=MESH,
     )
 
@@ -678,11 +723,13 @@
     def _():
         to_high.start()
 
-    def rest(c, carry):
-        landed(c)
-        return carry
-
-    lax.fori_loop(1, chunks, rest, 0)
+    lax.fori_loop(far_chunk + 1, chunks, land, 0)
+    for k in range(max(0, bands - 2), bands):
+        whole(k).wait()
+    if bands <= 2:
+        end(0).wait()
+    if bands <= 3:
+        end(1).wait()
 
     @pl.when(has_low)
     def _():
@@ -703,32 +750,44 @@
     lax.fori_loop(0, chunks, sent, 0)
 
 
-def exchange(tiles, loss, first, second, merge):
-    rows, local, cols = tiles.shape
+def advance(spectrum, near, mask, coef, loss, first, second, merge, periodic):
+    local, rows, cols = spectrum.shape
     peers = lax.axis_size("comp")
     depth = rows // peers
     chunks = depth // CHUNK
     comps, terms = merge.shape
-    tiles = tiles.reshape(depth, peers, local, cols)
+    stride = stride_of(local) + 8
     if peers == 8:
         order = [(1, 2, 3), (4, 5, 6, 7)]
     else:
         order = [tuple(range(1, peers))]
+    sets, _ = group_sets(local, periodic)
     return pl.pallas_call(
-        functools.partial(exchange_kernel, order),
-        in_specs=[ANY, WHOLE, ANY, ANY, ANY],
-        out_specs=[ANY, ANY],
+        functools.partial(advance_kernel, order, periodic),
+        in_specs=[ANY, WHOLE, WHOLE, WHOLE, WHOLE, ANY, ANY, ANY],
+        out_specs=[ANY, ANY, ANY],
         out_shape=[
+            jax.ShapeDtypeStruct(((rows + 2) * stride, cols), F32),
             jax.ShapeDtypeStruct((depth, peers, local, cols), BF16),
             jax.ShapeDtypeStruct((2, local, cols), BF16),
         ],
         scratch_shapes=[
+            VMEM((4, 16, rows, cols), BF16),
+            VMEM(((rows + 2 * HALO + 2) * stride, cols), F32),
+            VMEM(((SPAN + 2) * stride, cols), F32),
+            VMEM(((SPAN + 2) * stride, cols), F32),
+            VMEM((2 * (SPAN - RUN) * stride, cols), F32),
+            VMEM((RUN * len(sets[0]), 8, cols), F32),
+            VMEM((depth, peers, local, cols), BF16),
             VMEM((chunks, CHUNK, comps, cols), BF16),
             VMEM((chunks, CHUNK, comps, cols), BF16),
             VMEM((terms, comps), BF16),
             VMEM((terms, comps), BF16),
             VMEM((comps, terms), BF16),
             VMEM((terms, CHUNK * cols), BF16),
+            DMA((4,)),
+            DMA((rows // BAND,)),
+            DMA((2,)),
             DMA((3,)),
             DMA,
             DMA((chunks,)),
@@ -741,122 +800,131 @@
             flops=6 * comps * terms * depth * cols, bytes_accessed=6 * comps * terms, transcendentals=0
         ),
         compiler_params=pltpu.CompilerParams(
-            collective_id=2, has_side_effects=True, vmem_limit_bytes=60 * 1024 * 1024
+            collective_id=2, has_side_effects=True, vmem_limit_bytes=63 * 1024 * 1024
         ),
-        name="exchange",
-    )(tiles, loss, first, second, merge)
-
-
-def close_kernel(periodic, ends, density, back, edge, wind, mask, coef, out, cells, incs, staged, sems, out_sems):
+        name="advance",
+    )(spectrum, near, mask, coef, loss, first, second, merge)
+
+
+def close_kernel(periodic, ends, density, back, edge, wind, mask, coef, out, cells, forced, turned, incs, side, staged, sems, out_sems):
     comps, rows, cols = staged.shape
-    stride = cells.shape[0] // (rows + 2)
-    block = 16
-    blocks = comps // block
-    turned = cells.reshape(rows + 2, stride, cols)
-    source = density.reshape(rows + 2, stride, cols)
+    stride = stride_of(comps) + 8
+    sets, ways = group_sets(comps, periodic)
+    size = len(sets[0])
+    bands = rows // BAND
+    views = [ref.reshape(rows + 2, stride, cols) for ref in (density, cells)]
 
     def fetches(b):
-        at = pl.ds(pl.multiple_of(b * block, block), block)
+        at = pl.ds(sets[b][0] * 8, size * 8)
         moves = [
-            (source.at[:, at], turned.at[:, at]),
+            (views[0].at[:, at], views[1].at[:, at]),
             (edge.at[0, at], incs.at[0, at]),
-            (back.at[0, at], incs.at[1, at]),
-            (back.at[pl.ds(2, rows - 2), at], incs.at[pl.ds(2, rows - 2), at]),
-            (back.at[1, at], incs.at[rows, at]),
+            (back.at[pl.ds(0, BAND), at], incs.at[pl.ds(1, BAND), at]),
             (edge.at[1, at], incs.at[rows + 1, at]),
         ]
+        if bands > 1:
+            moves.append((back.at[pl.ds(BAND, BAND), at], incs.at[pl.ds(rows + 1 - BAND, BAND), at]))
+        if bands > 2:
+            between = rows - 2 * BAND
+            moves.append((back.at[pl.ds(2 * BAND, between), at], incs.at[pl.ds(1 + BAND, between), at]))
         return [pltpu.make_async_copy(src, dst, sems.at[b, k]) for k, (src, dst) in enumerate(moves)]
 
-    def give(b):
-        at = pl.ds(b * block, block)
-        return pltpu.make_async_copy(staged.at[at], out.at[at], out_sems.at[b])
-
-    for b in range(blocks):
+    for b in range(len(sets)):
         for f in fetches(b):
             f.start()
 
-    for b in range(blocks):
+    run = max(k for k in range(1, 17) if (rows + 2) % k == 0)
+    trips = (rows + 2) // run
+
+    def at(row, g):
+        return pl.ds(pl.multiple_of(row * stride + g * 8, 8), 8)
+
+    def set_of(b):
+        group_set = sets[b]
         for f in fetches(b):
             f.wait()
-        span = slice(b * block, (b + 1) * block)
-        for side, at in ((0, 0), (1, rows + 1)):
-
-            @pl.when(ends[side] == 1)
-            def _(at=at, span=span):
-                incs[at, span, :] = jnp.zeros((block, cols), BF16)
-
-        pair = [2 * b, 2 * b + 1]
-        ways = [directions([8 * g + k for k in range(8)], periodic) for g in pair]
-        factor = [[coef[k, pl.ds(g * 8, 8), :] for k in range(8)] for g in pair]
-
-        def one(i, state):
-            both = incs[i, span, :].astype(F32)
-            blow, turn_x, turn_y = wind[0, i], wind[1, i], wind[2, i]
-            sea = mask[i - 1]
-            fresh = []
-            for j, g in enumerate(pair):
-                c, w, e, s, n, rate, cos_h, sin_h = factor[j]
-                west, east, south, north = ways[j]
-                here, past = state[j]
-                at = pl.multiple_of(i * stride + g * 8, 8)
-                d = cells[pl.ds(at, 8), :]
-                facing = jnp.maximum(cos_h * turn_x + sin_h * turn_y, 0.0)
-                growth = rate * blow * (facing * facing)
-                new = d + growth * d + both[j * 8 : (j + 1) * 8]
-                v = c * here
-                if west:
-                    v = v + w * pltpu.roll(here, 1, 1)
-                if east:
-                    v = v + e * pltpu.roll(here, cols - 1, 1)
-                if south:
-                    v = v + s * past
-                if north:
-                    v = v + n * new
-                back_at = pl.multiple_of((i - 1) * stride + g * 8, 8)
-                cells[pl.ds(back_at, 8), :] = v * sea
-                fresh.append((new, here))
-            return tuple(fresh)
-
-        def first(i):
-            both = incs[i, span, :].astype(F32)
+        span = pl.ds(group_set[0] * 8, size * 8)
+        for end, row in ((0, 0), (1, rows + 1)):
+
+            @pl.when(ends[end] == 1)
+            def _(row=row):
+                incs[row, span, :] = jnp.zeros((size * 8, cols), BF16)
+
+        factor = {g: [coef[k, pl.ds(g * 8, 8), :] for k in range(8)] for g in group_set}
+
+        def ahead(row):
             made = []
-            for j, g in enumerate(pair):
-                rate, cos_h, sin_h = factor[j][5:8]
-                d = cells[pl.ds(i * stride + g * 8, 8), :]
-                facing = jnp.maximum(cos_h * wind[1, i] + sin_h * wind[2, i], 0.0)
-                growth = rate * wind[0, i] * (facing * facing)
-                made.append((d + growth * d + both[j * 8 : (j + 1) * 8], jnp.zeros((8, cols), F32)))
-            return tuple(made)
-
-        def two(t, state):
-            return one(2 * t + 2, one(2 * t + 1, state))
-
-        state = lax.fori_loop(0, (rows + 1) // 2, two, first(0))
-        if (rows + 1) % 2:
-            one(rows + 1, state)
-
-    def finish_block(b, carry):
-        def lift(k, carry):
-            c = b * block + k
-            staged[c] = cells[pl.ds(stride + c, rows, stride=stride), :].astype(BF16)
+            for r in range(run):
+                blow, turn_x, turn_y = wind[0, row + r], wind[1, row + r], wind[2, row + r]
+                for g in group_set:
+                    if g % 2 == 0:
+                        both = incs[row + r, pl.ds(g * 8, 16), :].astype(F32)
+                    rate, cos_h, sin_h = factor[g][5:8]
+                    d = cells[at(row + r, g), :]
+                    facing = jnp.maximum(cos_h * turn_x + sin_h * turn_y, 0.0)
+                    growth = rate * blow * (facing * facing)
+                    new = d + growth * d + both[(g % 2) * 8 : (g % 2) * 8 + 8]
+                    forced[at(row + r + 1, g), :] = new
+                    west, east = ways[g][:2]
+                    made.append(column_terms(new, factor[g][1], factor[g][2], west, east))
+            return made
+
+        def keep(made):
+            for k, v in enumerate(made):
+                side[k] = v
+
+        def finish(row):
+            for j, g in enumerate(group_set):
+                c, _, _, s, n = factor[g][:5]
+                south, north = ways[g][2:]
+                held = forced[at(row, g), :] if south else None
+                here = forced[at(row + 1, g), :]
+                for r in range(run):
+                    after = forced[at(row + r + 2, g), :] if north or r < run - 1 else None
+                    v = c * here + side[r * size + j]
+                    if south:
+                        v = v + s * held
+                    if north:
+                        v = v + n * after
+                    turned[at(row + r, g), :] = v * mask[row + r]
+                    held, here = here, after
+
+        def trip(t, carry):
+            made = ahead((t + 1) * run)
+            finish(t * run)
+            keep(made)
             return carry
 
-        lax.fori_loop(0, block, lift, 0)
+        keep(ahead(0))
+        lax.fori_loop(0, trips - 1, trip, 0)
+        finish((trips - 1) * run)
+
+    def give(b):
+        part = pl.ds(b * size * 8, size * 8)
+        return pltpu.make_async_copy(staged.at[part], out.at[part], out_sems.at[b])
+
+    zeros = jnp.zeros((stride, cols), F32)
+    forced[pl.ds(0, stride), :] = zeros
+    forced[pl.ds((rows + 3) * stride, stride), :] = zeros
+    for b in range(len(sets)):
+        set_of(b)
+
+        def lift(k, carry, b=b):
+            c = b * size * 8 + k
+            staged[c] = turned[pl.ds(stride + c, rows, stride=stride), :].astype(BF16)
+            return carry
+
+        lax.fori_loop(0, size * 8, lift, 0)
         give(b).start()
-        return carry
-
-    lax.fori_loop(0, blocks, finish_block, 0)
-
-    def drain(b, carry):
+    for b in range(len(sets)):
         give(b).wait()
-        return carry
-
-    lax.fori_loop(0, blocks, drain, 0)
 
 
 def close(density, back, edge, wind, mask, coef, ends, periodic):
     rows, comps, cols = back.shape
     stride = stride_of(comps) + 8
+    sets, _ = group_sets(comps, periodic)
+    run = max(k for k in range(1, 17) if (rows + 2) % k == 0)
     return pl.pallas_call(
         functools.partial(close_kernel, periodic),
         in_specs=[pl.BlockSpec(memory_space=SMEM), ANY, ANY, ANY, WHOLE, WHOLE, WHOLE],
@@ -864,25 +932,27 @@
         out_shape=jax.ShapeDtypeStruct((comps, rows, cols), BF16),
         scratch_shapes=[
             VMEM(((rows + 2) * stride, cols), F32),
+            VMEM(((rows + 4) * stride, cols), F32),
+            VMEM(((rows + 2) * stride, cols), F32),
             VMEM((rows + 2, comps, cols), BF16),
+            VMEM((run * len(sets[0]), 8, cols), F32),
             VMEM((comps, rows, cols), BF16),
-            DMA((comps // 16, 6)),
-            DMA((comps // 16,)),
+            DMA((len(sets), 6)),
+            DMA((len(sets),)),
         ],
-        compiler_params=pltpu.CompilerParams(vmem_limit_bytes=48 * 1024 * 1024),
+        compiler_params=pltpu.CompilerParams(vmem_limit_bytes=56 * 1024 * 1024),
         name="close",
     )(ends, density, back, edge, wind, mask, coef)
 
 
-def tall(rows_of, lead):
-    rows_of = jnp.pad(rows_of, ((lead, lead), (0, 0)))
+def tall(rows_of):
     return jnp.broadcast_to(rows_of[:, None, :], (rows_of.shape[0], 8, rows_of.shape[1]))
 
 
 def body(spectrum, land_mask, wind_speed, wind_dir, input_rate, dissipation, pair_first, pair_second, merge_weight):
     local, rows, cols = spectrum.shape
     peers = lax.axis_size("comp")
-    fits = local % 16 == 0 and rows % (peers * CHUNK) == 0 and rows % 16 == 0 and cols == 128
+    fits = local % 16 == 0 and rows % BAND == 0 and BAND % (peers * CHUNK) == 0 and cols == 128
     if not fits:
         return plain_body(
             spectrum, land_mask, wind_speed, wind_dir, input_rate, dissipation, pair_first, pair_second, merge_weight
@@ -902,16 +972,17 @@
     coef = jnp.broadcast_to(coef[:, :, None], (8, local, cols))
 
     sea = jnp.concatenate([near_mask[0], land_mask, near_mask[1]]).astype(F32)
-    sea = tall(sea, PAD)
+    sea = tall(sea)
     angle = jnp.concatenate([near_angle[0, HALO - 1 :], wind_dir, near_angle[1, :1]])
     speed = jnp.concatenate([near_speed[0, HALO - 1 :], wind_speed, near_speed[1, :1]])
-    wind = jnp.stack([tall(speed, 0), tall(jnp.cos(angle), 0), tall(jnp.sin(angle), 0)])
+    wind = jnp.stack([tall(speed), tall(jnp.cos(angle)), tall(jnp.sin(angle))])
     geo = lax.axis_index("geo")
     ends = jnp.stack([geo == 0, geo == lax.axis_size("geo") - 1]).astype(jnp.int32)
 
-    density, tiles = spread(spectrum, near, sea, coef, periodic)
-    back, edge = exchange(tiles, dissipation[:, None], pair_first, pair_second, merge_weight)
-    below = PAD + HALO - 1
+    density, back, edge = advance(
+        spectrum, near, sea, coef, dissipation[:, None], pair_first, pair_second, merge_weight, periodic
+    )
+    below = HALO - 1
     return close(density, back.reshape(rows, local, cols), edge, wind, sea[below : below + rows + 2], coef, ends, periodic)
 
 

time: 380 us -> 263 us (0.69)
  Pallas kernels: 367 us -> 247 us
    pallas_call x2 -> x1, Pallas kernels: 306 us -> 226 us  [advance(): pl.pallas_call(functools.partial(advance_kernel, order, periodic), in_spe...]
    pallas_call x1, Pallas kernels: 56.1 us -> 15.9 us  [close(): pl.pallas_call(functools.partial(close_kernel, periodic), in_specs=[pl.Bl...]
where the time goes in v2:
time: 263 us; the launch traced here: 261 us
  Pallas kernels  247 us (94%)
  local copies, waits for them, and re-layouts  11.7 us (4%)
    pallas_call x1, Pallas kernels, advance(): pl.pallas_call(functools.partial(advance_kernel, order, periodic), in_spe...  226 us
    pallas_call x1, Pallas kernels, close(): pl.pallas_call(functools.partial(close_kernel, periodic), in_specs=[pl.Bl...  15.9 us
    unnamed x11, local copies, waits for them, and re-layouts  6.37 us
    pallas_call x1, Pallas kernels, geo_halo(): pl.pallas_call(geo_halo_kernel, in_specs=[ANY] * 4, out_specs=[WHOLE] * 4...  5.38 us

profile of v2, /device:TPU:0, one launch (start us, length us, event | category | flops | bytes accessed | tf_op | source)
XLA Modules:
  0.0 261.2 jit_solution(3617688971086583359)
XLA Ops:
  0.0 0.0 copy-start
  0.0 0.0 copy-start.4
  0.0 0.0 copy-start.3
  0.0 0.6 add_convert_fusion.1.ends
  0.6 5.4 %geo_halo.1 = (bf16[2,144,8,128]{3,2,1,0:T(8,128)(2,1)}, s32[2,8,128]{2,1,0:T(8,128)}, f32[2,8,128]{2,1,0:T(8,128)}, f32[2,8,128]{2,1,0:T(8,128)}) custom-call(bf16[144,128,128]{2,1,0:T(8,128)(2,1)} %spectrum.3, s32[128,128]{1,0:T(8,128)} %mask.1, f32[128,128]{1,0:T(8,128)} %speed.1, f32[128,128]{1,0:T(8,128)} %angle.1), custom_call_target="tpu_custom_call" | custom-call | tf_op jit(solution)/shard_map/geo_halo/pallas_call | solution.py:369
  6.0 0.7 slice_bitcast_fusion.2
  6.7 0.0 copy-done
  6.7 0.9 broadcast_in_dim.8.mask
  7.6 0.1 multiply_maximum_fusion
  7.6 0.1 multiply_maximum_fusion.3
  7.7 0.1 multiply_maximum_fusion.1
  7.8 0.1 fusion.8
  7.9 0.0 copy-done.4
  7.9 1.0 broadcast_in_dim.9.coef
  8.9 0.0 copy-done.3
  8.9 1.0 broadcast_in_dim.24.loss
  10.0 6.3 %copy.12.merge_in = bf16[1152,1728]{1,0:T(8,128)(2,1)} copy(bf16[1152,1728]{0,1:T(8,128)(2,1)} %param.17) | data formatting | bytes 7962624 | tf_op args[8]
  16.3 0.0 copy-start.1
  16.3 0.0 copy-start.2
  16.3 225.7 %advance.1 = (f32[19760,128]{1,0:T(8,128)}, bf16[16,8,144,128]{3,2,1,0:T(8,128)(2,1)}, bf16[2,144,128]{2,1,0:T(8,128)(2,1)}) custom-call(bf16[144,128,128]{2,1,0:T(8,128)(2,1)} %spectrum.3, bf16[2,144,8,128]{3,2,1,0:T(8,128)(2,1)} %get-tuple-element.12.near, f32[144,8,128]{2,1,0:T(8,128)} %broadcast_in_dim.8.mask, f32[8,144,128]{2,1,0:T(8,128)} %broadcast_in_dim.9.coef, ...), custom_call_target="tpu_custom_call" | custom-call | flops 24461180928 | bytes 11943936 | tf_op jit(solution)/shard_map/advance/pallas_call | solution.py:765
  242.0 0.7 slice_bitcast_fusion.5
  242.7 0.0 copy-done.1
  242.7 0.3 fusion.3
  243.1 0.0 copy-done.2
  243.2 1.2 pad_maximum_fusion.wind
  244.4 0.8 broadcast_in_dim.11.mask
  245.3 15.9 %close.1 = bf16[144,128,128]{2,1,0:T(8,128)(2,1)} custom-call(s32[2]{0:T(128)} %add_convert_fusion.1.ends, f32[19760,128]{1,0:T(8,128)} %get-tuple-element.14.density, bf16[128,144,128]{2,1,0:T(8,128)(2,1)} %bitcast.23, bf16[2,144,128]{2,1,0:T(8,128)(2,1)} %get-tuple-element.16.edge, f32[3,130,8,128]{3,2,1,0:T(8,128)} %pad_maximum_fusion.wind, ...), custom_call_target="tpu_custom_call" | custom-call | tf_op jit(solution)/shard_map/close/pallas_call | solution.py:928
  (7 shorter events, 0.2 us)
Async XLA Ops:
  0.0 6.7 %copy-start = (s32[128,128]{1,0:T(8,128)S(1)}, s32[128,128]{1,0:T(8,128)}, u32[]{:S(2)}) copy-start(s32[128,128]{1,0:T(8,128)} %mask.1) | copy-start | bytes 196612
  0.0 7.9 %copy-start.4 = (f32[144]{0:T(256)S(1)}, f32[144]{0:T(256)}, u32[]{:S(2)}) copy-start(f32[144]{0:T(256)} %param.13) | copy-start | bytes 1732
  0.0 8.9 %copy-start.3 = (f32[1152]{0:T(1024)S(1)}, f32[1152]{0:T(1024)}, u32[]{:S(2)}) copy-start(f32[1152]{0:T(1024)} %param.14) | copy-start | bytes 13828
  16.3 226.4 %copy-start.1 = (f32[128,128]{1,0:T(8,128)S(1)}, f32[128,128]{1,0:T(8,128)}, u32[]{:S(2)}) copy-start(f32[128,128]{1,0:T(8,128)} %angle.1) | copy-start | bytes 196612
  16.3 226.8 %copy-start.2 = (f32[128,128]{1,0:T(8,128)S(1)}, f32[128,128]{1,0:T(8,128)}, u32[]{:S(2)}) copy-start(f32[128,128]{1,0:T(8,128)} %speed.1) | copy-start | bytes 196612

commit v3 on v2

--- a/solution.py
+++ b/solution.py
@@ -22,6 +22,8 @@
 DMA = pltpu.SemaphoreType.DMA
 CHUNK = 2
 BAND = 32
+BLOCK = 16
+TILES = 13
 RUN = 12
 SPAN = BAND + 2 * HALO
 SMEM = pltpu.SMEM
@@ -296,21 +298,21 @@
     return finish(coef, density, low, high, wind, mask, incs, HALO)
 
 
-def geo_halo_kernel(spectrum, mask, speed, angle, near, near_mask, near_speed, near_angle, send, recv):
+def geo_halo_kernel(spectrum, mask, speed, angle, near, near_mask, near_speed, near_angle, seas, send, recv, sea_send, sea_recv):
     geo, ends = lax.axis_index("geo"), lax.axis_size("geo") - 1
     rows = spectrum.shape[1]
     barrier = pltpu.get_barrier_semaphore()
     has_low, has_high = geo > 0, geo < ends
-
-    @pl.when(has_low)
-    def _():
-        pl.semaphore_signal(barrier, inc=1, device_id={"geo": geo - 1}, device_id_type=MESH)
-
-    @pl.when(has_high)
-    def _():
-        pl.semaphore_signal(barrier, inc=1, device_id={"geo": geo + 1}, device_id_type=MESH)
-
-    pl.semaphore_wait(barrier, jnp.minimum(geo, 1) + jnp.minimum(ends - geo, 1))
+    others = [lax.rem(geo + k, ends + 1) for k in range(1, ends + 1)]
+    for who in others:
+        pl.semaphore_signal(barrier, inc=1, device_id={"geo": who}, device_id_type=MESH)
+    pl.semaphore_wait(barrier, ends)
+
+    def whole_mask(k):
+        return pltpu.make_async_remote_copy(
+            src_ref=mask, dst_ref=seas.at[geo], send_sem=sea_send.at[k], recv_sem=sea_recv.at[k],
+            device_id={"geo": others[k]}, device_id_type=MESH,
+        )
 
     def copies(side):
         at = pl.ds(0, HALO) if side else pl.ds(rows - HALO, HALO)
@@ -341,6 +343,11 @@
         for c in up:
             c.start()
 
+    for k in range(ends):
+        whole_mask(k).start()
+    own = pltpu.make_async_copy(mask, seas.at[geo], sea_send.at[ends])
+    own.start()
+
     for side, missing in ((0, geo == 0), (1, geo == ends)):
 
         @pl.when(missing)
@@ -362,16 +369,22 @@
         for c in down:
             c.wait_recv()
 
+    for k in range(ends):
+        whole_mask(k).wait()
+    own.wait()
+
 
 def geo_halo(spectrum, mask, speed, angle):
     comps, _, cols = spectrum.shape
+    count = lax.axis_size("geo")
     flat = lambda a: jax.ShapeDtypeStruct((2, HALO, cols), a.dtype)
+    seas = jax.ShapeDtypeStruct((count,) + mask.shape, mask.dtype)
     return pl.pallas_call(
         geo_halo_kernel,
         in_specs=[ANY] * 4,
-        out_specs=[WHOLE] * 4,
-        out_shape=[jax.ShapeDtypeStruct((2, comps, HALO, cols), spectrum.dtype), flat(mask), flat(speed), flat(angle)],
-        scratch_shapes=[DMA((2, 4)), DMA((2, 4))],
+        out_specs=[WHOLE] * 5,
+        out_shape=[jax.ShapeDtypeStruct((2, comps, HALO, cols), spectrum.dtype), flat(mask), flat(speed), flat(angle), seas],
+        scratch_shapes=[DMA((2, 4)), DMA((2, 4)), DMA((count,)), DMA((count,))],
         compiler_params=pltpu.CompilerParams(collective_id=1, has_side_effects=True),
         name="geo_halo",
     )(spectrum, mask, speed, angle)
@@ -517,13 +530,53 @@
     return other
 
 
-def advance_kernel(
-    order, periodic, spectrum, near, mask, coef, loss, first_in, second_in, merge_in, density, back, edge,
-    staged, field, work_a, work_b, done, side, tiles,
-    spectra, incs, first, second, merge, product,
-    stage_sems, density_sems, end_sems,
-    weight_sems, send_sem, recv_sem, return_sem, back_sem, edge_send, edge_recv,
-):
+def one_hot(pos, first, count):
+    cols = pos.shape[1]
+    slot = lax.broadcasted_iota(jnp.int32, (count, cols), 0) + first
+    at = jnp.broadcast_to(pos[None], (count // 8, 8, cols)).reshape(count, cols)
+    return jnp.where(slot == at, 1.0, 0.0).astype(BF16)
+
+
+def squeeze_block(rows_of, pos, at, factor, tiles, start, peers):
+    count, _, cols = rows_of.shape
+    for n in range(0, TILES, 2):
+        wide = min(2, TILES - n)
+        lanes = slice(n * cols, count * cols)
+        for q in range(n, count):
+            factor[: wide * cols, q * cols : (q + 1) * cols] = one_hot(pos[at + q], n * cols, wide * cols)
+        x = jnp.concatenate([rows_of[q] for q in range(n, count)], axis=1)
+        moved = lax.dot_general(
+            x, factor[: wide * cols, lanes], (((1,), (1,)), ((), ())), preferred_element_type=F32
+        ).astype(BF16)
+        for h in range(wide):
+            t = start + n + h
+            tiles[lax.div(t, peers), lax.rem(t, peers)] = moved[:, h * cols : (h + 1) * cols]
+
+
+def widen_rows(tiles, start, peers, pos, at, first, count, factor):
+    cols = factor.shape[1] // 2
+    reach = min(first + count, TILES)
+    for n in range(reach):
+        for q in range(count):
+            factor[n * cols : (n + 1) * cols, q * cols : (q + 1) * cols] = one_hot(pos[at + q], n * cols, cols)
+    x = []
+    for n in range(reach):
+        t = start + n
+        x.append(tiles[lax.div(t, peers), lax.rem(t, peers)])
+    x = jnp.concatenate(x, axis=1) if reach > 1 else x[0]
+    return jnp.dot(x, factor[: reach * cols, : count * cols], preferred_element_type=F32).astype(BF16)
+
+
+def advance_kernel(order, periodic, squeeze, spectrum, near, mask, coef, loss, first_in, second_in, merge_in, *refs):
+    if squeeze:
+        pos, edge_pos, *refs = refs
+    density, back, edge, *refs = refs
+    staged, field, work_a, work_b, done, side, tiles, spectra, incs, first, second, merge, merge_part, product, *refs = refs
+    if squeeze:
+        rows_of, home, edge_in, edge_out, flat, gather, spread, flat_sems, *refs = refs
+    else:
+        home = back
+    stage_sems, density_sems, end_sems, weight_sems, send_sem, recv_sem, return_sem, back_sem, edge_send, edge_recv = refs
     peers = lax.axis_size("comp")
     me = lax.axis_index("comp")
     geo, ends = lax.axis_index("geo"), lax.axis_size("geo") - 1
@@ -544,8 +597,6 @@
     def _():
         pl.semaphore_signal(barrier, inc=1, device_id={"geo": geo + 1}, device_id_type=MESH)
 
-    pl.semaphore_wait(barrier, peers - 1 + jnp.minimum(geo, 1) + jnp.minimum(ends - geo, 1))
-
     def part(who):
         return pl.ds(pl.multiple_of(who * local, 16), local)
 
@@ -560,7 +611,7 @@
     def homeward(c, who):
         return pltpu.make_async_remote_copy(
             src_ref=incs.at[c, :, part(who)],
-            dst_ref=back.at[pl.ds(c * width, width), me],
+            dst_ref=home.at[pl.ds(c * width, width), me],
             send_sem=return_sem, recv_sem=back_sem.at[c],
             device_id={"comp": who}, device_id_type=MESH,
         )
@@ -570,7 +621,7 @@
 
     loads = [
         pltpu.make_async_copy(src, dst, weight_sems.at[k])
-        for k, (src, dst) in enumerate(((first_in, first), (second_in, second), (merge_in, merge)))
+        for k, (src, dst) in enumerate(((first_in, first), (second_in, second)))
     ]
     rows = mask.shape[0] - 2 * HALO
     stride = stride_of(local) + 8
@@ -582,48 +633,55 @@
     for work in (work_a, work_b):
         work[pl.ds(0, stride), :] = zeros
         work[pl.ds((SPAN + 1) * stride, stride), :] = zeros
+    pl.semaphore_wait(barrier, peers - 1 + jnp.minimum(geo, 1) + jnp.minimum(ends - geo, 1))
 
     sets, ways = group_sets(local, periodic)
 
     def whole(k):
-        at = lax.rem(k, 2) * (SPAN - RUN)
-        band = band_at(k, bands)
         return pltpu.make_async_copy(
-            done.at[pl.ds((at + 2) * stride, BAND * stride)],
-            density.at[pl.ds((band * BAND + 1) * stride, BAND * stride)],
+            done.at[pl.ds(2 * stride, BAND * stride)],
+            density.at[pl.ds((band_at(k, bands) * BAND + 1) * stride, BAND * stride)],
             density_sems.at[k],
         )
 
-    def end(side_of):
-        k = 1 if side_of and bands > 1 else 0
-        at = (k % 2) * (SPAN - RUN) + (BAND + 2 if side_of else 1)
-        row = rows + 1 if side_of else 0
+    def end(far):
+        row = rows + 1 if far else 0
         return pltpu.make_async_copy(
-            done.at[pl.ds(at * stride, stride)], density.at[pl.ds(row * stride, stride)], end_sems.at[side_of]
+            done.at[pl.ds((BAND + 2 if far else 1) * stride, stride)],
+            density.at[pl.ds(row * stride, stride)],
+            end_sems.at[far],
         )
+
+    far_band = min(1, bands - 1)
+
+    def settle(k):
+        whole(k).wait()
+
+        @pl.when(k == 0)
+        def _():
+            end(0).wait()
+
+        @pl.when(k == far_band)
+        def _():
+            end(1).wait()
+
+    def ready(k):
+        return lax.div(k * (rows // bands * TILES // BLOCK if squeeze else BAND), peers * width)
+
+    def needed(k):
+        return lax.div(k * (BAND // BLOCK * TILES) + peers * width - 1, peers * width)
 
     def form(k, carry):
         band = band_at(k, bands)
-        at = lax.rem(k, 2) * (SPAN - RUN)
-
-        @pl.when(k >= 2)
+
+        @pl.when(k > 0)
         def _():
-            whole(k - 2).wait()
-
-        @pl.when(k == 2)
-        def _():
-            end(0).wait()
-
-        if bands > 3:
-
-            @pl.when(k == 3)
-            def _():
-                end(1).wait()
+            settle(k - 1)
 
         for group_set in sets:
             substeps(
                 field, (work_a, work_b), done, mask, coef, side, group_set, ways,
-                band * BAND, band * BAND + 1, at, stride,
+                band * BAND, band * BAND + 1, 0, stride,
             )
         whole(k).start()
 
@@ -631,28 +689,76 @@
         def _():
             end(0).start()
 
-        @pl.when(k == min(1, bands - 1))
+        @pl.when(k == far_band)
         def _():
             end(1).start()
 
-        def pack(r, carry):
-            t = k * BAND + r
-            from_at = pl.multiple_of((at + 2 + r) * stride, 8)
-            tiles[lax.div(t, peers), lax.rem(t, peers)] = done[pl.ds(from_at, local), :].astype(BF16)
+        if squeeze:
+
+            def block(b, carry):
+                def pack(q, carry):
+                    r = b * BLOCK + q
+                    r = jnp.where(k == 1, BAND - 1 - r, r)
+                    from_at = pl.multiple_of((2 + r) * stride, 8)
+                    rows_of[q] = done[pl.ds(from_at, local), :].astype(BF16)
+                    return carry
+
+                lax.fori_loop(0, BLOCK, pack, 0)
+                whole_block = k * (BAND // BLOCK) + b
+                squeeze_block(rows_of, pos, whole_block * BLOCK, gather, tiles, whole_block * TILES, peers)
+                return carry
+
+            lax.fori_loop(0, BAND // BLOCK, block, 0)
+        else:
+
+            def pack(r, carry):
+                t = k * BAND + r
+                from_at = pl.multiple_of((2 + r) * stride, 8)
+                tiles[lax.div(t, peers), lax.rem(t, peers)] = done[pl.ds(from_at, local), :].astype(BF16)
+                return carry
+
+            lax.fori_loop(0, BAND, pack, 0)
+
+        for group in order:
+
+            def launch(c, carry, group=group):
+                for who in group:
+                    outward(c, partner(me, who, peers)).start()
+                return carry
+
+            lax.fori_loop(ready(k), ready(k + 1), launch, 0)
+
+        def own(c, carry):
+            for h in range(width):
+                spectra[c, h, part(me), :] = tiles[c * width + h, me]
             return carry
 
-        lax.fori_loop(0, BAND, pack, 0)
-        per = BAND // (peers * width)
-        for group in order:
-            for j in range(per):
-                for who in group:
-                    outward(k * per + j, partner(me, who, peers)).start()
-        for j in range(per):
-            for h in range(width):
-                spectra[k * per + j, h, part(me), :] = tiles[(k * per + j) * width + h, me]
+        lax.fori_loop(ready(k), ready(k + 1), own, 0)
         return carry
 
     lax.fori_loop(0, bands, form, 0)
+
+    def fetch(m):
+        slot = lax.rem(m, 2)
+        return pltpu.make_async_copy(
+            merge_in.at[:, pl.ds(pl.multiple_of(m * cols, cols), cols)], merge_part.at[slot], weight_sems.at[2 + slot]
+        )
+
+    fetch(0).start()
+
+    def flip(m, carry):
+        @pl.when(m + 1 < comps // cols)
+        def _():
+            fetch(m + 1).start()
+
+        fetch(m).wait()
+        to = pl.ds(pl.multiple_of(m * cols, cols), cols)
+        for t in range(0, terms, cols):
+            size = min(cols, terms - t)
+            merge[to, t : t + size] = merge_part[lax.rem(m, 2), t : t + size, :].T
+        return carry
+
+    lax.fori_loop(0, comps // cols, flip, 0)
     for load in loads:
         load.wait()
 
@@ -663,15 +769,12 @@
         arrived = spectra.at[c, :, pl.ds(0, comps - local)]
         pltpu.make_async_copy(arrived, arrived, recv_sem.at[c]).wait()
 
-        def both():
-            return jnp.concatenate([spectra[c, h] for h in range(width)], axis=1)
-
         def multiply(t, carry):
-            rows = pl.ds(pl.multiple_of(t * tile, 16), tile)
-            x = both()
-            one = jnp.dot(first[rows, :], x, preferred_element_type=F32)
-            two = jnp.dot(second[rows, :], x, preferred_element_type=F32)
-            product[rows, :] = (one * two).astype(BF16)
+            at = pl.ds(pl.multiple_of(t * tile, 16), tile)
+            x = jnp.concatenate([spectra[c, h] for h in range(width)], axis=1) if width > 1 else spectra[c, 0]
+            one = jnp.dot(first[at, :], x, preferred_element_type=F32)
+            two = jnp.dot(second[at, :], x, preferred_element_type=F32)
+            product[at, :] = (one * two).astype(BF16)
             return carry
 
         lax.fori_loop(0, terms // tile, multiply, 0)
@@ -680,38 +783,43 @@
             energy = jnp.sum(spectra[c, h].astype(F32), axis=0, keepdims=True)
             roots.append(jnp.sqrt(energy / comps + 1e-06))
         for d in range(0, comps, step):
-            rows = slice(d, d + step)
-            moved = jnp.dot(merge[rows, :], product[...], preferred_element_type=F32)
+            at = slice(d, d + step)
+            moved = jnp.dot(merge[at, :], product[...], preferred_element_type=F32)
             for h in range(width):
                 lanes = slice(h * cols, (h + 1) * cols)
-                total = moved[:, lanes] - loss[rows, :] * roots[h] * spectra[c, h, rows, :].astype(F32)
-                incs[c, h, rows, :] = total.astype(BF16)
+                total = moved[:, lanes] - loss[at, :] * roots[h] * spectra[c, h, at, :].astype(F32)
+                incs[c, h, at, :] = total.astype(BF16)
         for group in order:
             for k in group:
                 homeward(c, partner(me, k, peers)).start()
-        own_home(c).start()
+        if squeeze:
+            for h in range(width):
+                home[c * width + h, me] = incs[c, h, part(me), :]
+        else:
+            own_home(c).start()
         return carry
 
     lax.fori_loop(0, chunks, work, 0)
 
-    def landed(c):
-        there = back.at[pl.ds(c * width, width)]
+    def land(c, carry):
+        there = home.at[pl.ds(c * width, width), pl.ds(0, peers - 1 if squeeze else peers)]
         pltpu.make_async_copy(there, there, back_sem.at[c]).wait()
-
-    far_chunk = (min(2, bands) * BAND - 1) // (peers * width)
-
-    def land(c, carry):
-        landed(c)
         return carry
 
-    lax.fori_loop(0, far_chunk + 1, land, 0)
-    last = min(2, bands) * BAND - 1
+    if squeeze:
+        last = BAND // BLOCK * TILES
+    else:
+        last = min(2, bands) * BAND - 1
+    landed = last // (peers * width) + 1
+    lax.fori_loop(0, landed, land, 0)
+    arriving = edge_in if squeeze else edge
     to_low = pltpu.make_async_remote_copy(
-        src_ref=back.at[0, 0], dst_ref=edge.at[1], send_sem=edge_send.at[1], recv_sem=edge_recv.at[1],
+        src_ref=home.at[0, 0], dst_ref=arriving.at[1], send_sem=edge_send.at[1], recv_sem=edge_recv.at[1],
         device_id={"geo": geo - 1}, device_id_type=MESH,
     )
     to_high = pltpu.make_async_remote_copy(
-        src_ref=back.at[last // peers, last % peers], dst_ref=edge.at[0], send_sem=edge_send.at[0], recv_sem=edge_recv.at[0],
+        src_ref=home.at[last // peers, last % peers], dst_ref=arriving.at[0],
+        send_sem=edge_send.at[0], recv_sem=edge_recv.at[0],
         device_id={"geo": geo + 1}, device_id_type=MESH,
     )
 
@@ -723,23 +831,77 @@
     def _():
         to_high.start()
 
-    lax.fori_loop(far_chunk + 1, chunks, land, 0)
-    for k in range(max(0, bands - 2), bands):
-        whole(k).wait()
-    if bands <= 2:
-        end(0).wait()
-    if bands <= 3:
-        end(1).wait()
-
-    @pl.when(has_low)
-    def _():
-        to_low.wait_send()
-        to_high.wait_recv()
-
-    @pl.when(has_high)
-    def _():
-        to_high.wait_send()
-        to_low.wait_recv()
+    if not squeeze:
+        lax.fori_loop(landed, chunks, land, 0)
+    settle(bands - 1)
+
+    def edges_in():
+        @pl.when(has_low)
+        def _():
+            to_low.wait_send()
+            to_high.wait_recv()
+
+        @pl.when(has_high)
+        def _():
+            to_high.wait_send()
+            to_low.wait_recv()
+
+    if squeeze:
+
+        def put(k):
+            return pltpu.make_async_copy(
+                flat.at[lax.rem(k, 2)], back.at[pl.ds(k * BAND, BAND)], flat_sems.at[k]
+            )
+
+        def widen(k, carry):
+            lax.fori_loop(jnp.maximum(needed(k), landed), jnp.maximum(needed(k + 1), landed), land, 0)
+
+            @pl.when(k >= 2)
+            def _():
+                put(k - 2).wait()
+
+            def block(b, carry):
+                whole_block = k * (BAND // BLOCK) + b
+                for j in range(0, BLOCK, 2):
+                    made = widen_rows(
+                        home, whole_block * TILES, peers, pos, whole_block * BLOCK + j, j, 2, spread
+                    )
+                    for h in range(2):
+                        r = b * BLOCK + j + h
+                        r = jnp.where(k == 1, BAND - 1 - r, r)
+                        flat[lax.rem(k, 2), r] = made[:, h * cols : (h + 1) * cols]
+                return carry
+
+            lax.fori_loop(0, BAND // BLOCK, block, 0)
+            put(k).start()
+            return carry
+
+        def edge_put(which):
+            return pltpu.make_async_copy(edge_out.at[which], edge.at[which], end_sems.at[which])
+
+        @pl.when(geo == 0)
+        def _():
+            edge_in[0] = jnp.zeros((local, cols), BF16)
+
+        @pl.when(geo == ends)
+        def _():
+            edge_in[1] = jnp.zeros((local, cols), BF16)
+
+        lax.fori_loop(0, bands - 1, widen, 0)
+        edges_in()
+        for which in range(2):
+            spread[:cols, :cols] = one_hot(edge_pos[which], 0, cols)
+            edge_out[which] = jnp.dot(
+                edge_in[which], spread[:cols, :cols], preferred_element_type=F32
+            ).astype(BF16)
+            edge_put(which).start()
+        lax.fori_loop(bands - 1, bands, widen, 0)
+        for k in range(bands - 2, bands):
+            put(k).wait()
+        for which in range(2):
+            edge_put(which).wait()
+    else:
+        edges_in()
 
     def sent(c, carry):
         for k in range(1, peers):
@@ -750,11 +912,13 @@
     lax.fori_loop(0, chunks, sent, 0)
 
 
-def advance(spectrum, near, mask, coef, loss, first, second, merge, periodic):
+def advance(spectrum, near, mask, coef, loss, first, second, merge, places, periodic):
     local, rows, cols = spectrum.shape
     peers = lax.axis_size("comp")
-    depth = rows // peers
-    chunks = depth // CHUNK
+    squeeze = places is not None
+    width = 1 if squeeze else CHUNK
+    depth = (rows // BLOCK * TILES if squeeze else rows) // peers
+    chunks = depth // width
     comps, terms = merge.shape
     stride = stride_of(local) + 8
     if peers == 8:
@@ -762,33 +926,50 @@
     else:
         order = [tuple(range(1, peers))]
     sets, _ = group_sets(local, periodic)
-    return pl.pallas_call(
-        functools.partial(advance_kernel, order, periodic),
-        in_specs=[ANY, WHOLE, WHOLE, WHOLE, WHOLE, ANY, ANY, ANY],
+    extra = []
+    if squeeze:
+        extra = [
+            VMEM((BLOCK, local, cols), BF16),
+            VMEM((depth, peers, local, cols), BF16),
+            VMEM((2, local, cols), BF16),
+            VMEM((2, local, cols), BF16),
+            VMEM((2, BAND, local, cols), BF16),
+            VMEM((2 * cols, BLOCK * cols), BF16),
+            VMEM((TILES * cols, 2 * cols), BF16),
+            DMA((rows // BAND,)),
+        ]
+    back_shape = (rows, local, cols) if squeeze else (depth, peers, local, cols)
+    density, back, edge = pl.pallas_call(
+        functools.partial(advance_kernel, order, periodic, squeeze),
+        in_specs=[ANY, WHOLE, WHOLE, WHOLE, WHOLE, ANY, ANY, ANY] + ([WHOLE, WHOLE] if squeeze else []),
         out_specs=[ANY, ANY, ANY],
         out_shape=[
             jax.ShapeDtypeStruct(((rows + 2) * stride, cols), F32),
-            jax.ShapeDtypeStruct((depth, peers, local, cols), BF16),
+            jax.ShapeDtypeStruct(back_shape, BF16),
             jax.ShapeDtypeStruct((2, local, cols), BF16),
         ],
         scratch_shapes=[
-            VMEM((4, 16, rows, cols), BF16),
+            VMEM((2, 16, rows, cols), BF16),
             VMEM(((rows + 2 * HALO + 2) * stride, cols), F32),
             VMEM(((SPAN + 2) * stride, cols), F32),
             VMEM(((SPAN + 2) * stride, cols), F32),
-            VMEM((2 * (SPAN - RUN) * stride, cols), F32),
+            VMEM(((SPAN - RUN) * stride, cols), F32),
             VMEM((RUN * len(sets[0]), 8, cols), F32),
             VMEM((depth, peers, local, cols), BF16),
-            VMEM((chunks, CHUNK, comps, cols), BF16),
-            VMEM((chunks, CHUNK, comps, cols), BF16),
+            VMEM((chunks, width, comps, cols), BF16),
+            VMEM((chunks, width, comps, cols), BF16),
             VMEM((terms, comps), BF16),
             VMEM((terms, comps), BF16),
             VMEM((comps, terms), BF16),
-            VMEM((terms, CHUNK * cols), BF16),
-            DMA((4,)),
+            VMEM((2, terms, cols), BF16),
+            VMEM((terms, width * cols), BF16),
+        ]
+        + extra
+        + [
+            DMA((2,)),
             DMA((rows // BAND,)),
             DMA((2,)),
-            DMA((3,)),
+            DMA((4,)),
             DMA,
             DMA((chunks,)),
             DMA,
@@ -800,10 +981,25 @@
             flops=6 * comps * terms * depth * cols, bytes_accessed=6 * comps * terms, transcendentals=0
         ),
         compiler_params=pltpu.CompilerParams(
-            collective_id=2, has_side_effects=True, vmem_limit_bytes=63 * 1024 * 1024
+            collective_id=3 if squeeze else 2, has_side_effects=True, vmem_limit_bytes=67043328
         ),
-        name="advance",
-    )(spectrum, near, mask, coef, loss, first, second, merge)
+        name="advance_sea" if squeeze else "advance_all",
+    )(spectrum, near, mask, coef, loss, first, second, merge.T, *(places or ()))
+    return density, back.reshape(rows, local, cols), edge
+
+
+def sea_places(sea, near_low, near_high):
+    rows, cols = sea.shape
+    bands = rows // BAND
+    parts = [sea[:BAND], jnp.flip(sea[rows - BAND :], axis=0), sea[BAND : rows - BAND]]
+    sea = jnp.concatenate(parts)
+    steps = jnp.triu(jnp.ones((cols, cols), F32))
+    inner = jnp.dot(jnp.concatenate([sea, near_low, near_high]), steps)
+    total = inner[:rows, cols - 1].reshape(rows // BLOCK, BLOCK)
+    before = jnp.dot(total, jnp.triu(jnp.ones((BLOCK, BLOCK), F32), 1))
+    place = jnp.where(sea > 0, inner[:rows] + before.reshape(rows, 1), 0.0) - 1.0
+    edge = jnp.where(jnp.concatenate([near_low, near_high]) > 0, inner[rows:], 0.0) - 1.0
+    return tall(place.astype(jnp.int32)), tall(edge.astype(jnp.int32))
 
 
 def close_kernel(periodic, ends, density, back, edge, wind, mask, coef, out, cells, forced, turned, incs, side, staged, sems, out_sems):
@@ -958,7 +1154,7 @@
             spectrum, land_mask, wind_speed, wind_dir, input_rate, dissipation, pair_first, pair_second, merge_weight
         )
     periodic = local % ND == 0
-    near, near_mask, near_speed, near_angle = geo_halo(spectrum, land_mask, wind_speed, wind_dir)
+    near, near_mask, near_speed, near_angle, seas = geo_halo(spectrum, land_mask, wind_speed, wind_dir)
 
     ids = lax.axis_index("comp") * local + jnp.arange(local, dtype=jnp.int32)
     frequency = (ids // ND).astype(F32)
@@ -979,11 +1175,19 @@
     geo = lax.axis_index("geo")
     ends = jnp.stack([geo == 0, geo == lax.axis_size("geo") - 1]).astype(jnp.int32)
 
-    density, back, edge = advance(
-        spectrum, near, sea, coef, dissipation[:, None], pair_first, pair_second, merge_weight, periodic
-    )
+    given = (spectrum, near, sea, coef, dissipation[:, None], pair_first, pair_second, merge_weight)
+    whole = lambda *a: advance(*a[:8], None, periodic)
+    packed = lambda *a: advance(*a[:8], a[8:], periodic)
+    count = rows // BLOCK * TILES
+    if rows >= 2 * BAND and BLOCK == 16 and count % peers == 0 and local % 16 == 0:
+        near_sea = near_mask.astype(F32)
+        places = sea_places(land_mask.astype(F32), near_sea[0, HALO - 1 :], near_sea[1, :1])
+        held = jnp.sum(seas.reshape(-1, BLOCK * cols), axis=1)
+        density, back, edge = lax.cond(jnp.max(held) <= TILES * cols, packed, whole, *given, *places)
+    else:
+        density, back, edge = whole(*given)
     below = HALO - 1
-    return close(density, back.reshape(rows, local, cols), edge, wind, sea[below : below + rows + 2], coef, ends, periodic)
+    return close(density, back, edge, wind, sea[below : below + rows + 2], coef, ends, periodic)
 
 
 def solution(mesh):

time: 263 us -> 245 us (0.932)
  Pallas kernels: 247 us -> 226 us
  other arithmetic: 2.42 us -> 8.03 us
    pallas_call x2, Pallas kernels: 231 us -> 210 us  [the longest x1 199 us: advance(): pl.pallas_call(functools.partial(advance_kernel, order, periodic, squeeze...]
    unnamed x11 -> x16, local copies, waits for them, and re-layouts: 6.37 us -> 0.03 us
    broadcast_in_dim x2 -> x4, local copies, waits for them, and re-layouts: 1.7 us -> 4.58 us  [tall(): jnp.broadcast_to(rows_of[:, None, :], (rows_of.shape[0], 8, rows_of.shape...]
where the time goes in v3:
time: 245 us
  Pallas kernels  226 us (92%)
  local copies, waits for them, and re-layouts  9.42 us (4%)
  other arithmetic  8.03 us (3%)
    pallas_call x1, Pallas kernels, advance(): pl.pallas_call(functools.partial(advance_kernel, order, periodic, squeeze...  199 us
    pallas_call x1, Pallas kernels, close(): pl.pallas_call(functools.partial(close_kernel, periodic), in_specs=[pl.Bl...  15.8 us
    pallas_call x1, Pallas kernels, geo_halo(): pl.pallas_call(geo_halo_kernel, in_specs=[ANY] * 4, out_specs=[WHOLE] * 5...  11.1 us

profile of v3, /device:TPU:0, one launch (start us, length us, event | category | flops | bytes accessed | tf_op | source)
XLA Modules:
  0.0 244.6 jit_solution(10926995506942560854)
XLA Ops:
  0.0 11.1 %geo_halo.1 = (bf16[2,144,8,128]{3,2,1,0:T(8,128)(2,1)}, s32[2,8,128]{2,1,0:T(8,128)}, f32[2,8,128]{2,1,0:T(8,128)}, f32[2,8,128]{2,1,0:T(8,128)}, s32[4,128,128]{2,1,0:T(8,128)}) custom-call(bf16[144,128,128]{2,1,0:T(8,128)(2,1)} %spectrum.1, s32[128,128]{1,0:T(8,128)} %mask.1, f32[128,128]{1,0:T(8,128)} %speed.1, f32[128,128]{1,0:T(8,128)} %angle.1), custom_call_target="tpu_custom_call" | custom-call | tf_op jit(solution)/shard_map/geo_halo/pallas_call | solution.py:382
  11.2 0.7 convert_element_type.97
  12.0 0.2 fusion.5
  12.2 0.2 slice_reduce_fusion
  12.4 0.1 reshape_squeeze.3
  12.5 0.1 fusion.12
  12.6 0.1 add.124
  12.7 0.7 fusion.4
  13.4 0.6 fusion.17
  13.9 0.1 multiply_maximum_fusion
  14.0 0.1 multiply_maximum_fusion.1
  14.1 0.1 multiply_maximum_fusion.3
  14.2 0.1 fusion.22
  14.3 1.0 broadcast_in_dim.25.coef
  15.3 1.3 slice_bitcast_fusion.2
  16.6 0.9 broadcast_in_dim.24
  17.4 1.1 reduce_sum.10
  18.5 0.1 reduce_sum.14
  18.6 0.1 reduce_sum.18
  18.7 0.7 reduce_max.9
  20.1 202.9 %conditional.1 = ((f32[19760,128]{1,0:T(8,128)}, bf16[128,144,128]{2,1,0:T(8,128)(2,1)}, bf16[2,144,128]{2,1,0:T(8,128)(2,1)})) conditional(s32[]{:T(128)} %convert_element_type.92, (bf16[1152,1728]{0,1:T(8,128)(2,1)}, bf16[144,128,128]{2,1,0:T(8,128)(2,1)}, bf16[2,144,8,128]{3,2,1,0:T(8,128)(2,1)}, f32[144,8,128]{2,1,0:T(8,128)}, ...), branch_computations={%region_3.4_spmd, %region_4.5_spmd} | conditional | flops 24461180928 | bytes 12552200 | solution.py:1186
  20.1 1.1 copy.11.loss
  21.2 1.7 broadcast_in_dim.53.refs_0_
  22.8 1.2 broadcast_in_dim.54.refs_1_
  24.0 198.7 %advance_sea.1 = (f32[19760,128]{1,0:T(8,128)}, bf16[128,144,128]{2,1,0:T(8,128)(2,1)}, bf16[2,144,128]{2,1,0:T(8,128)(2,1)}) custom-call(bf16[144,128,128]{2,1,0:T(8,128)(2,1)} %get-tuple-element.52.spectrum, bf16[2,144,8,128]{3,2,1,0:T(8,128)(2,1)} %get-tuple-element.53.near, f32[144,8,128]{2,1,0:T(8,128)} %get-tuple-element.54.mask, ...), custom_call_target="tpu_custom_call" | custom-call | flops 19874709504 | bytes 11943936 | tf_op jit(solution)/shard_map/cond/branch_1_fun/advance_sea/pallas_call | solution.py:942
  223.0 0.8 slice_bitcast_fusion.7
  223.8 1.1 fusion.8
  225.0 0.9 pad_maximum_fusion.1
  225.9 1.3 pad_maximum_fusion.wind
  227.2 0.8 broadcast_in_dim.52.mask
  228.0 0.7 add_convert_fusion.1.ends
  228.7 15.8 %close.1 = bf16[144,128,128]{2,1,0:T(8,128)(2,1)} custom-call(s32[2]{0:T(128)} %add_convert_fusion.1.ends, f32[19760,128]{1,0:T(8,128)} %get-tuple-element.73.density, bf16[128,144,128]{2,1,0:T(8,128)(2,1)} %get-tuple-element.74.back, bf16[2,144,128]{2,1,0:T(8,128)(2,1)S(1)} %copy-done.3, f32[3,130,8,128]{3,2,1,0:T(8,128)} %pad_maximum_fusion.wind, ...), custom_call_target="tpu_custom_call" | custom-call | tf_op jit(solution)/shard_map/close/pallas_call | solution.py:1124
  (30 shorter events, 0.3 us)
Async XLA Ops:
  0.0 11.9 %copy-start.1 = (s32[128,128]{1,0:T(8,128)S(1)}, s32[128,128]{1,0:T(8,128)}, u32[]{:S(2)}) copy-start(s32[128,128]{1,0:T(8,128)} %mask.1) | copy-start | bytes 196612
  0.0 14.2 %copy-start.7 = (f32[144]{0:T(256)S(1)}, f32[144]{0:T(256)}, u32[]{:S(2)}) copy-start(f32[144]{0:T(256)} %param.15) | copy-start | bytes 1732
  0.0 17.4 %copy-start.6 = (f32[1152]{0:T(1024)S(1)}, f32[1152]{0:T(1024)}, u32[]{:S(2)}) copy-start(f32[1152]{0:T(1024)} %param.16) | copy-start | bytes 13828
  223.0 4.2 %copy-start.2 = (s32[128,128]{1,0:T(8,128)S(1)}, s32[128,128]{1,0:T(8,128)}, u32[]{:S(2)}) copy-start(s32[128,128]{1,0:T(8,128)} %mask.1) | copy-start | bytes 196612
  223.0 4.2 %copy-start.4 = (s32[8,1,128]{2,0,1:T(8,128)S(1)}, s32[8,1,128]{2,0,1:T(8,128)}, u32[]{:S(2)}) copy-start(s32[8,1,128]{2,0,1:T(8,128)} %get-tuple-element.102) | copy-start | bytes 12292
  223.0 4.1 %copy-start.5 = (s32[8,1,128]{2,0,1:T(8,128)S(1)}, s32[8,1,128]{2,0,1:T(8,128)}, u32[]{:S(2)}) copy-start(s32[8,1,128]{2,0,1:T(8,128)} %get-tuple-element.103) | copy-start | bytes 12292
  223.0 5.7 %copy-start = (f32[8,144,128]{2,1,0:T(8,128)S(1)}, f32[8,144,128]{2,1,0:T(8,128)}, u32[]{:S(2)}) copy-start(f32[8,144,128]{2,1,0:T(8,128)} %broadcast_in_dim.25.coef) | copy-start | bytes 1769476
  223.0 5.6 %copy-start.3 = (bf16[2,144,128]{2,1,0:T(8,128)(2,1)S(1)}, bf16[2,144,128]{2,1,0:T(8,128)(2,1)}, u32[]{:S(2)}) copy-start(bf16[2,144,128]{2,1,0:T(8,128)(2,1)} %get-tuple-element.75.edge) | copy-start | bytes 221188

commit v4 on v3

--- a/solution.py
+++ b/solution.py
@@ -21,11 +21,12 @@
 MESH = pl.DeviceIdType.MESH
 DMA = pltpu.SemaphoreType.DMA
 CHUNK = 2
-BAND = 32
+BAND = 16
 BLOCK = 16
 TILES = 13
-RUN = 12
+RUN = 8
 SPAN = BAND + 2 * HALO
+OFF = HALO - RUN // 2
 SMEM = pltpu.SMEM
 
 
@@ -298,7 +299,9 @@
     return finish(coef, density, low, high, wind, mask, incs, HALO)
 
 
-def geo_halo_kernel(spectrum, mask, speed, angle, near, near_mask, near_speed, near_angle, seas, send, recv, sea_send, sea_recv):
+def geo_halo_kernel(
+    spectrum, mask, speed, angle, held, near, near_mask, near_speed, near_angle, seas, send, recv, sea_send, sea_recv
+):
     geo, ends = lax.axis_index("geo"), lax.axis_size("geo") - 1
     rows = spectrum.shape[1]
     barrier = pltpu.get_barrier_semaphore()
@@ -308,9 +311,9 @@
         pl.semaphore_signal(barrier, inc=1, device_id={"geo": who}, device_id_type=MESH)
     pl.semaphore_wait(barrier, ends)
 
-    def whole_mask(k):
+    def most(k):
         return pltpu.make_async_remote_copy(
-            src_ref=mask, dst_ref=seas.at[geo], send_sem=sea_send.at[k], recv_sem=sea_recv.at[k],
+            src_ref=held, dst_ref=seas.at[geo], send_sem=sea_send.at[k], recv_sem=sea_recv.at[k],
             device_id={"geo": others[k]}, device_id_type=MESH,
         )
 
@@ -344,8 +347,8 @@
             c.start()
 
     for k in range(ends):
-        whole_mask(k).start()
-    own = pltpu.make_async_copy(mask, seas.at[geo], sea_send.at[ends])
+        most(k).start()
+    own = pltpu.make_async_copy(held, seas.at[geo], sea_send.at[ends])
     own.start()
 
     for side, missing in ((0, geo == 0), (1, geo == ends)):
@@ -370,24 +373,24 @@
             c.wait_recv()
 
     for k in range(ends):
-        whole_mask(k).wait()
+        most(k).wait()
     own.wait()
 
 
-def geo_halo(spectrum, mask, speed, angle):
+def geo_halo(spectrum, mask, speed, angle, held):
     comps, _, cols = spectrum.shape
     count = lax.axis_size("geo")
     flat = lambda a: jax.ShapeDtypeStruct((2, HALO, cols), a.dtype)
-    seas = jax.ShapeDtypeStruct((count,) + mask.shape, mask.dtype)
+    seas = jax.ShapeDtypeStruct((count,) + held.shape, held.dtype)
     return pl.pallas_call(
         geo_halo_kernel,
-        in_specs=[ANY] * 4,
+        in_specs=[ANY] * 5,
         out_specs=[WHOLE] * 5,
         out_shape=[jax.ShapeDtypeStruct((2, comps, HALO, cols), spectrum.dtype), flat(mask), flat(speed), flat(angle), seas],
         scratch_shapes=[DMA((2, 4)), DMA((2, 4)), DMA((count,)), DMA((count,))],
         compiler_params=pltpu.CompilerParams(collective_id=1, has_side_effects=True),
         name="geo_halo",
-    )(spectrum, mask, speed, angle)
+    )(spectrum, mask, speed, angle, held)
 
 
 def directions(comps, periodic):
@@ -408,9 +411,9 @@
     return w * pltpu.roll(x, 1, 1) if west else e * pltpu.roll(x, cols - 1, 1)
 
 
-def group_sets(comps, periodic):
+def group_sets(comps, periodic, limit):
     groups = comps // 8
-    count = max(k for k in range(1, 7) if groups % k == 0)
+    count = max(k for k in range(1, limit + 1) if groups % k == 0)
     sets = [list(range(k * count, (k + 1) * count)) for k in range(groups // count)]
     ways = [directions([8 * g + k for k in range(8)], periodic) for g in range(groups)]
     return sets, ways
@@ -478,41 +481,99 @@
             keep(made)
 
 
-def turn_in(spectrum, near, staged, field, sems, stride):
-    comps, rows, cols = spectrum.shape
-    slots, block = staged.shape[:2]
-    blocks = comps // block
-    for at in (0, (rows + 2 * HALO + 1) * stride):
-        field[pl.ds(at, stride), :] = jnp.zeros((stride, cols), F32)
-
-    def fetch(b):
-        slot = lax.rem(b, slots)
-        return pltpu.make_async_copy(spectrum.at[pl.ds(b * block, block)], staged.at[slot], sems.at[slot])
-
-    for b in range(min(slots, blocks)):
-        fetch(b).start()
-
-    def turn(b, carry):
-        fetch(b).wait()
-        slot = lax.rem(b, slots)
-
-        def one(k, carry):
-            c = b * block + k
-            v = jnp.concatenate(
-                [near[0, c].astype(F32), staged[slot, k].astype(F32), near[1, c].astype(F32)], axis=0
-            )
-            field[pl.ds(stride + c, rows + 2 * HALO, stride=stride), :] = v
+class TurnIn:
+    def __init__(self, spectrum, near, staged, field, sems, stride, side):
+        self.spectrum, self.near, self.staged, self.field, self.sems = spectrum, near, staged, field, sems
+        self.stride, self.side = stride, side
+        comps, rows, _ = spectrum.shape
+        slots, self.block = staged.shape[:2]
+        self.blocks = comps // self.block
+        self.begin, self.count = (SPAN - HALO, rows + HALO - SPAN) if side else (0, SPAN - HALO)
+        self.per = 1 if side else rows // SPAN
+        self.live = min(self.blocks, slots * self.per)
+
+    def place(self, b):
+        turn = lax.rem(b, self.live)
+        return lax.div(turn, self.per), pl.multiple_of(lax.rem(turn, self.per) * SPAN, SPAN)
+
+    def fetch(self, b):
+        slot, row = self.place(b)
+        return pltpu.make_async_copy(
+            self.spectrum.at[pl.ds(b * self.block, self.block), pl.ds(self.begin, self.count)],
+            self.staged.at[slot, :, pl.ds(row, self.count)],
+            self.sems.at[lax.rem(b, self.live)],
+        )
+
+    def start(self):
+        for b in range(self.live):
+            self.fetch(b).start()
+
+    def finish(self):
+        side, stride, count = self.side, self.stride, self.count
+        rows, cols = self.spectrum.shape[1:]
+        to = SPAN + 1 if side else 1
+        zeros = jnp.zeros((stride, cols), F32)
+        for row in (rows + 2 * HALO + 1,) if side else (0, SPAN + 1):
+            self.field[pl.ds(row * stride, stride), :] = zeros
+
+        def turn(b, carry):
+            self.fetch(b).wait()
+            slot, row = self.place(b)
+
+            def one(k, carry):
+                c = b * self.block + k
+                inner = self.staged[slot, k, pl.ds(row, count), :].astype(F32)
+                outer = self.near[side, c].astype(F32)
+                v = jnp.concatenate([inner, outer] if side else [outer, inner], axis=0)
+                self.field[pl.ds(to * stride + c, count + HALO, stride=stride), :] = v
+                return carry
+
+            lax.fori_loop(0, self.block, one, 0)
+            if self.live < self.blocks:
+
+                @pl.when(b + self.live < self.blocks)
+                def _():
+                    self.fetch(b + self.live).start()
+
             return carry
 
-        lax.fori_loop(0, block, one, 0)
-
-        @pl.when(b + slots < blocks)
-        def _():
-            fetch(b + slots).start()
-
+        lax.fori_loop(0, self.blocks, turn, 0)
+
+
+def spread_rows(to, first, rows_of):
+    cols = rows_of.shape[1]
+
+    count = rows_of.shape[0]
+    unroll = max(k for k in range(1, 17) if count % k == 0)
+
+    def several(t, carry):
+        for u in range(unroll):
+            i = t * unroll + u
+            to[first + i] = jnp.broadcast_to(rows_of[pl.ds(i, 1), :].astype(F32), (8, cols))
         return carry
 
-    lax.fori_loop(0, blocks, turn, 0)
+    lax.fori_loop(0, count // unroll, several, 0)
+
+
+def find_places(land, near_land, places, edge_places):
+    rows, cols = land.shape
+    sea = land[...].astype(F32)
+    i = lax.broadcasted_iota(jnp.int32, (rows, rows), 0)
+    j = lax.broadcasted_iota(jnp.int32, (rows, rows), 1)
+    same = lax.shift_right_logical(i, 4) == lax.shift_right_logical(j, 4)
+    sooner = jnp.where(i >= rows - BAND, i - j, j - i) < 0
+    before = jnp.where(jnp.logical_and(same, sooner), 1.0, 0.0).astype(BF16)
+    k = lax.broadcasted_iota(jnp.int32, (cols, cols), 0)
+    n = lax.broadcasted_iota(jnp.int32, (cols, cols), 1)
+    steps = jnp.where(k <= n, 1.0, 0.0).astype(BF16)
+    inner = jnp.dot(sea.astype(BF16), steps, preferred_element_type=F32)
+    held = jnp.dot(before, sea.astype(BF16), preferred_element_type=F32).astype(BF16)
+    ahead = jnp.dot(held, jnp.ones((cols, cols), BF16), preferred_element_type=F32)
+    places[...] = jnp.where(sea > 0, inner + ahead - 1.0, -1.0).astype(jnp.int32)
+    for side in range(2):
+        sea = near_land[side].astype(F32)
+        inner = jnp.dot(sea.astype(BF16), steps, preferred_element_type=F32)
+        edge_places[side] = jnp.where(sea > 0, inner - 1.0, -1.0).astype(jnp.int32)
 
 
 def band_at(k, bands):
@@ -533,17 +594,18 @@
 def one_hot(pos, first, count):
     cols = pos.shape[1]
     slot = lax.broadcasted_iota(jnp.int32, (count, cols), 0) + first
-    at = jnp.broadcast_to(pos[None], (count // 8, 8, cols)).reshape(count, cols)
-    return jnp.where(slot == at, 1.0, 0.0).astype(BF16)
-
-
-def squeeze_block(rows_of, pos, at, factor, tiles, start, peers):
+    return jnp.where(slot == jnp.broadcast_to(pos, (count, cols)), 1.0, 0.0).astype(BF16)
+
+
+def squeeze_block(rows_of, places, row_at, factor, tiles, start, peers):
     count, _, cols = rows_of.shape
     for n in range(0, TILES, 2):
         wide = min(2, TILES - n)
         lanes = slice(n * cols, count * cols)
         for q in range(n, count):
-            factor[: wide * cols, q * cols : (q + 1) * cols] = one_hot(pos[at + q], n * cols, wide * cols)
+            factor[: wide * cols, q * cols : (q + 1) * cols] = one_hot(
+                places[pl.ds(row_at(q), 1), :], n * cols, wide * cols
+            )
         x = jnp.concatenate([rows_of[q] for q in range(n, count)], axis=1)
         moved = lax.dot_general(
             x, factor[: wide * cols, lanes], (((1,), (1,)), ((), ())), preferred_element_type=F32
@@ -553,12 +615,14 @@
             tiles[lax.div(t, peers), lax.rem(t, peers)] = moved[:, h * cols : (h + 1) * cols]
 
 
-def widen_rows(tiles, start, peers, pos, at, first, count, factor):
+def widen_rows(tiles, start, peers, places, row_at, first, count, factor):
     cols = factor.shape[1] // 2
     reach = min(first + count, TILES)
     for n in range(reach):
         for q in range(count):
-            factor[n * cols : (n + 1) * cols, q * cols : (q + 1) * cols] = one_hot(pos[at + q], n * cols, cols)
+            factor[n * cols : (n + 1) * cols, q * cols : (q + 1) * cols] = one_hot(
+                places[pl.ds(row_at(first + q), 1), :], n * cols, cols
+            )
     x = []
     for n in range(reach):
         t = start + n
@@ -567,13 +631,13 @@
     return jnp.dot(x, factor[: reach * cols, : count * cols], preferred_element_type=F32).astype(BF16)
 
 
-def advance_kernel(order, periodic, squeeze, spectrum, near, mask, coef, loss, first_in, second_in, merge_in, *refs):
+def advance_kernel(
+    order, periodic, squeeze, spectrum, near, land, near_land, coef, loss, first_in, second_in, merge_in, *refs
+):
+    density, back, edge, *refs = refs
+    mask, staged, field, work_a, work_b, done, side, tiles, spectra, incs, first, second, merge, merge_part, product, *refs = refs
     if squeeze:
-        pos, edge_pos, *refs = refs
-    density, back, edge, *refs = refs
-    staged, field, work_a, work_b, done, side, tiles, spectra, incs, first, second, merge, merge_part, product, *refs = refs
-    if squeeze:
-        rows_of, home, edge_in, edge_out, flat, gather, spread, flat_sems, *refs = refs
+        places, edge_places, rows_of, home, edge_in, edge_out, flat, gather, spread, flat_sems, *refs = refs
     else:
         home = back
     stage_sems, density_sems, end_sems, weight_sems, send_sem, recv_sem, return_sem, back_sem, edge_send, edge_recv = refs
@@ -623,23 +687,30 @@
         pltpu.make_async_copy(src, dst, weight_sems.at[k])
         for k, (src, dst) in enumerate(((first_in, first), (second_in, second)))
     ]
-    rows = mask.shape[0] - 2 * HALO
+    rows = land.shape[0]
     stride = stride_of(local) + 8
     bands = rows // BAND
-    turn_in(spectrum, near, staged, field, stage_sems, stride)
-    for load in loads:
-        load.start()
+    opening = TurnIn(spectrum, near, staged, field, stage_sems, stride, 0)
+    others = TurnIn(spectrum, near, staged, field, stage_sems, stride, 1)
+    opening.start()
+    spread_rows(mask, 0, near_land.at[0])
+    spread_rows(mask, HALO, land)
+    spread_rows(mask, rows + HALO, near_land.at[1])
+    if squeeze:
+        find_places(land, near_land, places, edge_places)
+    opening.finish()
+    others.start()
     zeros = jnp.zeros((stride, cols), F32)
     for work in (work_a, work_b):
         work[pl.ds(0, stride), :] = zeros
         work[pl.ds((SPAN + 1) * stride, stride), :] = zeros
     pl.semaphore_wait(barrier, peers - 1 + jnp.minimum(geo, 1) + jnp.minimum(ends - geo, 1))
 
-    sets, ways = group_sets(local, periodic)
+    sets, ways = group_sets(local, periodic, 9)
 
     def whole(k):
         return pltpu.make_async_copy(
-            done.at[pl.ds(2 * stride, BAND * stride)],
+            done.at[pl.ds(OFF * stride, BAND * stride)],
             density.at[pl.ds((band_at(k, bands) * BAND + 1) * stride, BAND * stride)],
             density_sems.at[k],
         )
@@ -647,7 +718,7 @@
     def end(far):
         row = rows + 1 if far else 0
         return pltpu.make_async_copy(
-            done.at[pl.ds((BAND + 2 if far else 1) * stride, stride)],
+            done.at[pl.ds((BAND + OFF if far else OFF - 1) * stride, stride)],
             density.at[pl.ds(row * stride, stride)],
             end_sems.at[far],
         )
@@ -677,6 +748,12 @@
         @pl.when(k > 0)
         def _():
             settle(k - 1)
+
+        @pl.when(k == 1)
+        def _():
+            others.finish()
+            for load in loads:
+                load.start()
 
         for group_set in sets:
             substeps(
@@ -696,16 +773,20 @@
         if squeeze:
 
             def block(b, carry):
+                def row_at(q):
+                    r = b * BLOCK + q
+                    return jnp.where(k == 1, BAND - 1 - r, r)
+
                 def pack(q, carry):
-                    r = b * BLOCK + q
-                    r = jnp.where(k == 1, BAND - 1 - r, r)
-                    from_at = pl.multiple_of((2 + r) * stride, 8)
+                    from_at = pl.multiple_of((OFF + row_at(q)) * stride, 8)
                     rows_of[q] = done[pl.ds(from_at, local), :].astype(BF16)
                     return carry
 
                 lax.fori_loop(0, BLOCK, pack, 0)
-                whole_block = k * (BAND // BLOCK) + b
-                squeeze_block(rows_of, pos, whole_block * BLOCK, gather, tiles, whole_block * TILES, peers)
+                squeeze_block(
+                    rows_of, places, lambda q: band * BAND + row_at(q), gather, tiles,
+                    (k * (BAND // BLOCK) + b) * TILES, peers,
+                )
                 return carry
 
             lax.fori_loop(0, BAND // BLOCK, block, 0)
@@ -713,7 +794,7 @@
 
             def pack(r, carry):
                 t = k * BAND + r
-                from_at = pl.multiple_of((2 + r) * stride, 8)
+                from_at = pl.multiple_of((OFF + r) * stride, 8)
                 tiles[lax.div(t, peers), lax.rem(t, peers)] = done[pl.ds(from_at, local), :].astype(BF16)
                 return carry
 
@@ -861,15 +942,17 @@
                 put(k - 2).wait()
 
             def block(b, carry):
-                whole_block = k * (BAND // BLOCK) + b
+                def row_at(q):
+                    r = b * BLOCK + q
+                    return jnp.where(k == 1, BAND - 1 - r, r)
+
                 for j in range(0, BLOCK, 2):
                     made = widen_rows(
-                        home, whole_block * TILES, peers, pos, whole_block * BLOCK + j, j, 2, spread
+                        home, (k * (BAND // BLOCK) + b) * TILES, peers, places,
+                        lambda q: band_at(k, bands) * BAND + row_at(q), j, 2, spread,
                     )
                     for h in range(2):
-                        r = b * BLOCK + j + h
-                        r = jnp.where(k == 1, BAND - 1 - r, r)
-                        flat[lax.rem(k, 2), r] = made[:, h * cols : (h + 1) * cols]
+                        flat[lax.rem(k, 2), row_at(j + h)] = made[:, h * cols : (h + 1) * cols]
                 return carry
 
             lax.fori_loop(0, BAND // BLOCK, block, 0)
@@ -890,7 +973,8 @@
         lax.fori_loop(0, bands - 1, widen, 0)
         edges_in()
         for which in range(2):
-            spread[:cols, :cols] = one_hot(edge_pos[which], 0, cols)
+            row = 0 if which else HALO - 1
+            spread[:cols, :cols] = one_hot(edge_places[which, row : row + 1, :], 0, cols)
             edge_out[which] = jnp.dot(
                 edge_in[which], spread[:cols, :cols], preferred_element_type=F32
             ).astype(BF16)
@@ -912,10 +996,9 @@
     lax.fori_loop(0, chunks, sent, 0)
 
 
-def advance(spectrum, near, mask, coef, loss, first, second, merge, places, periodic):
+def advance(squeeze, periodic, spectrum, near, land, near_land, coef, loss, first, second, merge):
     local, rows, cols = spectrum.shape
     peers = lax.axis_size("comp")
-    squeeze = places is not None
     width = 1 if squeeze else CHUNK
     depth = (rows // BLOCK * TILES if squeeze else rows) // peers
     chunks = depth // width
@@ -925,10 +1008,13 @@
         order = [(1, 2, 3), (4, 5, 6, 7)]
     else:
         order = [tuple(range(1, peers))]
-    sets, _ = group_sets(local, periodic)
+    slots = -(-(local // 16) // (rows // SPAN))
+    sets, _ = group_sets(local, periodic, 9)
     extra = []
     if squeeze:
         extra = [
+            VMEM((rows, cols), jnp.int32),
+            VMEM((2, HALO, cols), jnp.int32),
             VMEM((BLOCK, local, cols), BF16),
             VMEM((depth, peers, local, cols), BF16),
             VMEM((2, local, cols), BF16),
@@ -941,7 +1027,7 @@
     back_shape = (rows, local, cols) if squeeze else (depth, peers, local, cols)
     density, back, edge = pl.pallas_call(
         functools.partial(advance_kernel, order, periodic, squeeze),
-        in_specs=[ANY, WHOLE, WHOLE, WHOLE, WHOLE, ANY, ANY, ANY] + ([WHOLE, WHOLE] if squeeze else []),
+        in_specs=[ANY, WHOLE, WHOLE, WHOLE, WHOLE, WHOLE, ANY, ANY, ANY],
         out_specs=[ANY, ANY, ANY],
         out_shape=[
             jax.ShapeDtypeStruct(((rows + 2) * stride, cols), F32),
@@ -949,7 +1035,8 @@
             jax.ShapeDtypeStruct((2, local, cols), BF16),
         ],
         scratch_shapes=[
-            VMEM((2, 16, rows, cols), BF16),
+            VMEM((rows + 2 * HALO, 8, cols), F32),
+            VMEM((slots, 16, rows, cols), BF16),
             VMEM(((rows + 2 * HALO + 2) * stride, cols), F32),
             VMEM(((SPAN + 2) * stride, cols), F32),
             VMEM(((SPAN + 2) * stride, cols), F32),
@@ -966,7 +1053,7 @@
         ]
         + extra
         + [
-            DMA((2,)),
+            DMA((max(slots, local // 16),)),
             DMA((rows // BAND,)),
             DMA((2,)),
             DMA((4,)),
@@ -984,28 +1071,17 @@
             collective_id=3 if squeeze else 2, has_side_effects=True, vmem_limit_bytes=67043328
         ),
         name="advance_sea" if squeeze else "advance_all",
-    )(spectrum, near, mask, coef, loss, first, second, merge.T, *(places or ()))
+    )(spectrum, near, land, near_land, coef, loss, first, second, merge.T)
     return density, back.reshape(rows, local, cols), edge
 
 
-def sea_places(sea, near_low, near_high):
-    rows, cols = sea.shape
-    bands = rows // BAND
-    parts = [sea[:BAND], jnp.flip(sea[rows - BAND :], axis=0), sea[BAND : rows - BAND]]
-    sea = jnp.concatenate(parts)
-    steps = jnp.triu(jnp.ones((cols, cols), F32))
-    inner = jnp.dot(jnp.concatenate([sea, near_low, near_high]), steps)
-    total = inner[:rows, cols - 1].reshape(rows // BLOCK, BLOCK)
-    before = jnp.dot(total, jnp.triu(jnp.ones((BLOCK, BLOCK), F32), 1))
-    place = jnp.where(sea > 0, inner[:rows] + before.reshape(rows, 1), 0.0) - 1.0
-    edge = jnp.where(jnp.concatenate([near_low, near_high]) > 0, inner[rows:], 0.0) - 1.0
-    return tall(place.astype(jnp.int32)), tall(edge.astype(jnp.int32))
-
-
-def close_kernel(periodic, ends, density, back, edge, wind, mask, coef, out, cells, forced, turned, incs, side, staged, sems, out_sems):
+def close_kernel(
+    periodic, density, back, edge, speed, near_speed, angle, near_angle, land, near_land, coef, out,
+    mask, wind, lines, cells, forced, turned, incs, side, staged, sems, out_sems,
+):
     comps, rows, cols = staged.shape
     stride = stride_of(comps) + 8
-    sets, ways = group_sets(comps, periodic)
+    sets, ways = group_sets(comps, periodic, 6)
     size = len(sets[0])
     bands = rows // BAND
     views = [ref.reshape(rows + 2, stride, cols) for ref in (density, cells)]
@@ -1029,6 +1105,17 @@
         for f in fetches(b):
             f.start()
 
+    def surround(kind, middle, near, change):
+        for first, ref in ((0, near.at[0]), (HALO, middle), (rows + HALO, near.at[1])):
+            lines[pl.ds(first, ref.shape[0]), :] = change(ref[...].astype(F32))
+        spread_rows(kind, 0, lines.at[pl.ds(HALO - 1, rows + 2)])
+
+    surround(mask, land, near_land, lambda v: v)
+    surround(wind.at[0], speed, near_speed, lambda v: v)
+    surround(wind.at[1], angle, near_angle, jnp.cos)
+    surround(wind.at[2], angle, near_angle, jnp.sin)
+    geo = lax.axis_index("geo")
+
     run = max(k for k in range(1, 17) if (rows + 2) % k == 0)
     trips = (rows + 2) // run
 
@@ -1040,9 +1127,9 @@
         for f in fetches(b):
             f.wait()
         span = pl.ds(group_set[0] * 8, size * 8)
-        for end, row in ((0, 0), (1, rows + 1)):
-
-            @pl.when(ends[end] == 1)
+        for end, row in ((0, 0), (lax.axis_size("geo") - 1, rows + 1)):
+
+            @pl.when(geo == end)
             def _(row=row):
                 incs[row, span, :] = jnp.zeros((size * 8, cols), BF16)
 
@@ -1116,17 +1203,20 @@
         give(b).wait()
 
 
-def close(density, back, edge, wind, mask, coef, ends, periodic):
+def close(periodic, density, back, edge, *fields):
     rows, comps, cols = back.shape
     stride = stride_of(comps) + 8
-    sets, _ = group_sets(comps, periodic)
+    sets, _ = group_sets(comps, periodic, 6)
     run = max(k for k in range(1, 17) if (rows + 2) % k == 0)
     return pl.pallas_call(
         functools.partial(close_kernel, periodic),
-        in_specs=[pl.BlockSpec(memory_space=SMEM), ANY, ANY, ANY, WHOLE, WHOLE, WHOLE],
+        in_specs=[ANY] * 3 + [WHOLE] * len(fields),
         out_specs=ANY,
         out_shape=jax.ShapeDtypeStruct((comps, rows, cols), BF16),
         scratch_shapes=[
+            VMEM((rows + 2, 8, cols), F32),
+            VMEM((3, rows + 2, 8, cols), F32),
+            VMEM((rows + 2 * HALO, cols), F32),
             VMEM(((rows + 2) * stride, cols), F32),
             VMEM(((rows + 4) * stride, cols), F32),
             VMEM(((rows + 2) * stride, cols), F32),
@@ -1138,11 +1228,7 @@
         ],
         compiler_params=pltpu.CompilerParams(vmem_limit_bytes=56 * 1024 * 1024),
         name="close",
-    )(ends, density, back, edge, wind, mask, coef)
-
-
-def tall(rows_of):
-    return jnp.broadcast_to(rows_of[:, None, :], (rows_of.shape[0], 8, rows_of.shape[1]))
+    )(density, back, edge, *fields)
 
 
 def body(spectrum, land_mask, wind_speed, wind_dir, input_rate, dissipation, pair_first, pair_second, merge_weight):
@@ -1154,7 +1240,9 @@
             spectrum, land_mask, wind_speed, wind_dir, input_rate, dissipation, pair_first, pair_second, merge_weight
         )
     periodic = local % ND == 0
-    near, near_mask, near_speed, near_angle, seas = geo_halo(spectrum, land_mask, wind_speed, wind_dir)
+    held = jnp.max(jnp.sum(land_mask.reshape(-1, min(BLOCK, rows) * cols), axis=1))
+    held = jnp.broadcast_to(held, (8, cols))
+    near, near_mask, near_speed, near_angle, seas = geo_halo(spectrum, land_mask, wind_speed, wind_dir, held)
 
     ids = lax.axis_index("comp") * local + jnp.arange(local, dtype=jnp.int32)
     frequency = (ids // ND).astype(F32)
@@ -1167,27 +1255,18 @@
     coef = jnp.stack([center, west, east, south, north, input_rate, cos_h, sin_h])
     coef = jnp.broadcast_to(coef[:, :, None], (8, local, cols))
 
-    sea = jnp.concatenate([near_mask[0], land_mask, near_mask[1]]).astype(F32)
-    sea = tall(sea)
-    angle = jnp.concatenate([near_angle[0, HALO - 1 :], wind_dir, near_angle[1, :1]])
-    speed = jnp.concatenate([near_speed[0, HALO - 1 :], wind_speed, near_speed[1, :1]])
-    wind = jnp.stack([tall(speed), tall(jnp.cos(angle)), tall(jnp.sin(angle))])
-    geo = lax.axis_index("geo")
-    ends = jnp.stack([geo == 0, geo == lax.axis_size("geo") - 1]).astype(jnp.int32)
-
-    given = (spectrum, near, sea, coef, dissipation[:, None], pair_first, pair_second, merge_weight)
-    whole = lambda *a: advance(*a[:8], None, periodic)
-    packed = lambda *a: advance(*a[:8], a[8:], periodic)
-    count = rows // BLOCK * TILES
-    if rows >= 2 * BAND and BLOCK == 16 and count % peers == 0 and local % 16 == 0:
-        near_sea = near_mask.astype(F32)
-        places = sea_places(land_mask.astype(F32), near_sea[0, HALO - 1 :], near_sea[1, :1])
-        held = jnp.sum(seas.reshape(-1, BLOCK * cols), axis=1)
-        density, back, edge = lax.cond(jnp.max(held) <= TILES * cols, packed, whole, *given, *places)
+    given = (
+        spectrum, near, land_mask, near_mask, coef, dissipation[:, None], pair_first, pair_second, merge_weight
+    )
+    whole = functools.partial(advance, False, periodic)
+    packed = functools.partial(advance, True, periodic)
+    if rows >= 2 * BAND and rows // BLOCK * TILES % peers == 0:
+        density, back, edge = lax.cond(jnp.max(seas) <= TILES * cols, packed, whole, *given)
     else:
         density, back, edge = whole(*given)
-    below = HALO - 1
-    return close(density, back, edge, wind, sea[below : below + rows + 2], coef, ends, periodic)
+    return close(
+        periodic, density, back, edge, wind_speed, near_speed, wind_dir, near_angle, land_mask, near_mask, coef
+    )
 
 
 def solution(mesh):

time: 245 us -> 229 us (0.935)
  Pallas kernels: 226 us -> 219 us
  other arithmetic: 8.03 us -> 3.41 us
  local copies, waits for them, and re-layouts: 9.42 us -> 4.87 us
    pallas_call x1, Pallas kernels: 199 us -> 195 us  [advance(): pl.pallas_call(functools.partial(advance_kernel, order, periodic, squeeze...]
    broadcast_in_dim x4 -> x1, local copies, waits for them, and re-layouts: 4.58 us -> 1.28 us  [body(): held = jnp.broadcast_to(held, (8, cols))]
    convert_element_type x6 -> x0, other arithmetic: 2.65 us -> none  [the longest x2 1.28 us: sea_places(): return (tall(place.astype(jnp.int32)), tall(edge.astype(jnp.int32)))]
where the time goes in v4:
time: 229 us
  Pallas kernels  219 us (96%)
  local copies, waits for them, and re-layouts  4.87 us (2%)
  other arithmetic  3.41 us (1%)
    pallas_call x1, Pallas kernels, advance(): pl.pallas_call(functools.partial(advance_kernel, order, periodic, squeeze...  195 us
    pallas_call x1, Pallas kernels, close(): pl.pallas_call(functools.partial(close_kernel, periodic), in_specs=[ANY]...  15.5 us
    pallas_call x1, Pallas kernels, geo_halo(): pl.pallas_call(geo_halo_kernel, in_specs=[ANY] * 5, out_specs=[WHOLE] * 5...  9.13 us

profile of v4, /device:TPU:0, one launch (start us, length us, event | category | flops | bytes accessed | tf_op | source)
XLA Modules:
  0.0 228.6 jit_solution(7240907773563569273)
XLA Ops:
  0.0 0.9 reduce_sum.10
  0.9 0.1 fusion.4
  1.0 0.1 multiply_maximum_fusion
  1.1 0.1 multiply_maximum_fusion.1
  1.2 0.1 multiply_maximum_fusion.3
  1.2 0.7 stack.5
  1.9 0.1 reduce_sum.14
  2.0 0.1 reduce_sum.18
  2.1 0.7 reduce_max.18
  2.9 1.3 broadcast_in_dim.12.held
  4.1 0.7 broadcast_in_dim.14
  4.8 1.0 broadcast_in_dim.13.coef
  5.9 9.1 %geo_halo.1 = (bf16[2,144,8,128]{3,2,1,0:T(8,128)(2,1)}, s32[2,8,128]{2,1,0:T(8,128)}, f32[2,8,128]{2,1,0:T(8,128)}, f32[2,8,128]{2,1,0:T(8,128)}, s32[4,8,128]{2,1,0:T(8,128)}) custom-call(bf16[144,128,128]{2,1,0:T(8,128)(2,1)} %spectrum.1, s32[128,128]{1,0:T(8,128)} %land.1, f32[128,128]{1,0:T(8,128)} %speed.3, f32[128,128]{1,0:T(8,128)} %angle.3, ...), custom_call_target="tpu_custom_call" | custom-call | tf_op jit(solution)/shard_map/geo_halo/pallas_call | solution.py:385
  15.0 1.4 reduce_max.19
  17.0 196.0 %conditional.1 = ((f32[19760,128]{1,0:T(8,128)}, bf16[128,144,128]{2,1,0:T(8,128)(2,1)}, bf16[2,144,128]{2,1,0:T(8,128)(2,1)})) conditional(s32[]{:T(128)} %convert_element_type.63, (bf16[1152,1728]{0,1:T(8,128)(2,1)}, bf16[144,128,128]{2,1,0:T(8,128)(2,1)}, bf16[2,144,8,128]{3,2,1,0:T(8,128)(2,1)}, s32[128,128]{1,0:T(8,128)}, ...), branch_computations={%region_4.5_spmd, %region_5.6_spmd} | conditional | flops 24461180928 | bytes 11953184 | solution.py:1264
  17.0 1.1 copy.11.loss
  18.1 194.6 %advance_sea.1 = (f32[19760,128]{1,0:T(8,128)}, bf16[128,144,128]{2,1,0:T(8,128)(2,1)}, bf16[2,144,128]{2,1,0:T(8,128)(2,1)}) custom-call(bf16[144,128,128]{2,1,0:T(8,128)(2,1)} %get-tuple-element.53.spectrum, bf16[2,144,8,128]{3,2,1,0:T(8,128)(2,1)} %get-tuple-element.54.near, s32[128,128]{1,0:T(8,128)} %get-tuple-element.55.land, ...), custom_call_target="tpu_custom_call" | custom-call | flops 19874709504 | bytes 11943936 | tf_op jit(solution)/shard_map/cond/branch_1_fun/advance_sea/pallas_call | solution.py:1028
  213.0 15.5 %close.1 = bf16[144,128,128]{2,1,0:T(8,128)(2,1)} custom-call(f32[19760,128]{1,0:T(8,128)} %get-tuple-element.73.density, bf16[128,144,128]{2,1,0:T(8,128)(2,1)} %get-tuple-element.74.back, bf16[2,144,128]{2,1,0:T(8,128)(2,1)} %get-tuple-element.75.edge, f32[128,128]{1,0:T(8,128)} %speed.3, f32[2,8,128]{2,1,0:T(8,128)} %get-tuple-element.76.near_speed, ...), custom_call_target="tpu_custom_call" | custom-call | tf_op jit(solution)/shard_map/close/pallas_call | solution.py:1211

commit v5 on v4

--- a/solution.py
+++ b/solution.py
@@ -27,6 +27,7 @@
 RUN = 8
 SPAN = BAND + 2 * HALO
 OFF = HALO - RUN // 2
+LAG = 2
 SMEM = pltpu.SMEM
 
 
@@ -742,90 +743,11 @@
     def needed(k):
         return lax.div(k * (BAND // BLOCK * TILES) + peers * width - 1, peers * width)
 
-    def form(k, carry):
-        band = band_at(k, bands)
-
-        @pl.when(k > 0)
-        def _():
-            settle(k - 1)
-
-        @pl.when(k == 1)
-        def _():
-            others.finish()
-            for load in loads:
-                load.start()
-
-        for group_set in sets:
-            substeps(
-                field, (work_a, work_b), done, mask, coef, side, group_set, ways,
-                band * BAND, band * BAND + 1, 0, stride,
-            )
-        whole(k).start()
-
-        @pl.when(k == 0)
-        def _():
-            end(0).start()
-
-        @pl.when(k == far_band)
-        def _():
-            end(1).start()
-
-        if squeeze:
-
-            def block(b, carry):
-                def row_at(q):
-                    r = b * BLOCK + q
-                    return jnp.where(k == 1, BAND - 1 - r, r)
-
-                def pack(q, carry):
-                    from_at = pl.multiple_of((OFF + row_at(q)) * stride, 8)
-                    rows_of[q] = done[pl.ds(from_at, local), :].astype(BF16)
-                    return carry
-
-                lax.fori_loop(0, BLOCK, pack, 0)
-                squeeze_block(
-                    rows_of, places, lambda q: band * BAND + row_at(q), gather, tiles,
-                    (k * (BAND // BLOCK) + b) * TILES, peers,
-                )
-                return carry
-
-            lax.fori_loop(0, BAND // BLOCK, block, 0)
-        else:
-
-            def pack(r, carry):
-                t = k * BAND + r
-                from_at = pl.multiple_of((OFF + r) * stride, 8)
-                tiles[lax.div(t, peers), lax.rem(t, peers)] = done[pl.ds(from_at, local), :].astype(BF16)
-                return carry
-
-            lax.fori_loop(0, BAND, pack, 0)
-
-        for group in order:
-
-            def launch(c, carry, group=group):
-                for who in group:
-                    outward(c, partner(me, who, peers)).start()
-                return carry
-
-            lax.fori_loop(ready(k), ready(k + 1), launch, 0)
-
-        def own(c, carry):
-            for h in range(width):
-                spectra[c, h, part(me), :] = tiles[c * width + h, me]
-            return carry
-
-        lax.fori_loop(ready(k), ready(k + 1), own, 0)
-        return carry
-
-    lax.fori_loop(0, bands, form, 0)
-
     def fetch(m):
         slot = lax.rem(m, 2)
         return pltpu.make_async_copy(
             merge_in.at[:, pl.ds(pl.multiple_of(m * cols, cols), cols)], merge_part.at[slot], weight_sems.at[2 + slot]
         )
-
-    fetch(0).start()
 
     def flip(m, carry):
         @pl.when(m + 1 < comps // cols)
@@ -839,9 +761,11 @@
             merge[to, t : t + size] = merge_part[lax.rem(m, 2), t : t + size, :].T
         return carry
 
-    lax.fori_loop(0, comps // cols, flip, 0)
-    for load in loads:
-        load.wait()
+    def weights():
+        fetch(0).start()
+        lax.fori_loop(0, comps // cols, flip, 0)
+        for load in loads:
+            load.wait()
 
     tile = max(t for t in range(16, 600, 16) if terms % t == 0)
     step = max(g for g in range(1, peers + 1) if peers % g == 0 and g * local <= 600) * local
@@ -880,7 +804,92 @@
             own_home(c).start()
         return carry
 
-    lax.fori_loop(0, chunks, work, 0)
+    def form(k, carry):
+        band = band_at(k, bands)
+
+        @pl.when(k > 0)
+        def _():
+            settle(k - 1)
+
+        @pl.when(k == 1)
+        def _():
+            others.finish()
+            for load in loads:
+                load.start()
+
+        for group_set in sets:
+            substeps(
+                field, (work_a, work_b), done, mask, coef, side, group_set, ways,
+                band * BAND, band * BAND + 1, 0, stride,
+            )
+        whole(k).start()
+
+        @pl.when(k == 0)
+        def _():
+            end(0).start()
+
+        @pl.when(k == far_band)
+        def _():
+            end(1).start()
+
+        if squeeze:
+
+            def block(b, carry):
+                def row_at(q):
+                    r = b * BLOCK + q
+                    return jnp.where(k == 1, BAND - 1 - r, r)
+
+                def pack(q, carry):
+                    from_at = pl.multiple_of((OFF + row_at(q)) * stride, 8)
+                    rows_of[q] = done[pl.ds(from_at, local), :].astype(BF16)
+                    return carry
+
+                lax.fori_loop(0, BLOCK, pack, 0)
+                squeeze_block(
+                    rows_of, places, lambda q: band * BAND + row_at(q), gather, tiles,
+                    (k * (BAND // BLOCK) + b) * TILES, peers,
+                )
+                return carry
+
+            lax.fori_loop(0, BAND // BLOCK, block, 0)
+        else:
+
+            def pack(r, carry):
+                t = k * BAND + r
+                from_at = pl.multiple_of((OFF + r) * stride, 8)
+                tiles[lax.div(t, peers), lax.rem(t, peers)] = done[pl.ds(from_at, local), :].astype(BF16)
+                return carry
+
+            lax.fori_loop(0, BAND, pack, 0)
+
+        for group in order:
+
+            def launch(c, carry, group=group):
+                for who in group:
+                    outward(c, partner(me, who, peers)).start()
+                return carry
+
+            lax.fori_loop(ready(k), ready(k + 1), launch, 0)
+
+        def own(c, carry):
+            for h in range(width):
+                spectra[c, h, part(me), :] = tiles[c * width + h, me]
+            return carry
+
+        lax.fori_loop(ready(k), ready(k + 1), own, 0)
+
+        @pl.when(k == LAG)
+        def _():
+            weights()
+
+        lax.fori_loop(ready(jnp.maximum(k - LAG, 0)), ready(jnp.maximum(k - LAG + 1, 0)), work, 0)
+        return carry
+
+    lax.fori_loop(0, bands, form, 0)
+    if bands <= LAG:
+        weights()
+
+    lax.fori_loop(ready(max(bands - LAG, 0)), chunks, work, 0)
 
     def land(c, carry):
         there = home.at[pl.ds(c * width, width), pl.ds(0, peers - 1 if squeeze else peers)]
@@ -1234,7 +1243,7 @@
 def body(spectrum, land_mask, wind_speed, wind_dir, input_rate, dissipation, pair_first, pair_second, merge_weight):
     local, rows, cols = spectrum.shape
     peers = lax.axis_size("comp")
-    fits = local % 16 == 0 and rows % BAND == 0 and BAND % (peers * CHUNK) == 0 and cols == 128
+    fits = local % 16 == 0 and rows % BAND == 0 and rows >= 2 * BAND and BAND % (peers * CHUNK) == 0 and cols == 128
     if not fits:
         return plain_body(
             spectrum, land_mask, wind_speed, wind_dir, input_rate, dissipation, pair_first, pair_second, merge_weight

time: 229 us -> 233 us (1.017)
  Pallas kernels: 219 us -> 223 us
    pallas_call x1, Pallas kernels: 195 us -> 198 us  [advance(): pl.pallas_call(functools.partial(advance_kernel, order, periodic, squeeze...]
where the time goes in v5:
time: 233 us; the launch traced here: 232 us
  Pallas kernels  223 us (96%)
  local copies, waits for them, and re-layouts  4.87 us (2%)
  other arithmetic  3.41 us (1%)
    pallas_call x1, Pallas kernels, advance(): pl.pallas_call(functools.partial(advance_kernel, order, periodic, squeeze...  198 us
    pallas_call x1, Pallas kernels, close(): pl.pallas_call(functools.partial(close_kernel, periodic), in_specs=[ANY]...  15.5 us
    pallas_call x1, Pallas kernels, geo_halo(): pl.pallas_call(geo_halo_kernel, in_specs=[ANY] * 5, out_specs=[WHOLE] * 5...  9.13 us

profile of v5, /device:TPU:0, one launch (start us, length us, event | category | flops | bytes accessed | tf_op | source)
XLA Modules:
  0.0 232.2 jit_solution(17707438705035315532)
XLA Ops:
  0.0 0.9 reduce_sum.10
  0.9 0.1 fusion.4
  1.0 0.1 multiply_maximum_fusion
  1.1 0.1 multiply_maximum_fusion.1
  1.2 0.1 multiply_maximum_fusion.3
  1.2 0.7 stack.5
  1.9 0.1 reduce_sum.14
  2.0 0.1 reduce_sum.18
  2.1 0.7 reduce_max.18
  2.9 1.3 broadcast_in_dim.12.held
  4.1 0.7 broadcast_in_dim.14
  4.8 1.0 broadcast_in_dim.13.coef
  5.9 9.1 %geo_halo.1 = (bf16[2,144,8,128]{3,2,1,0:T(8,128)(2,1)}, s32[2,8,128]{2,1,0:T(8,128)}, f32[2,8,128]{2,1,0:T(8,128)}, f32[2,8,128]{2,1,0:T(8,128)}, s32[4,8,128]{2,1,0:T(8,128)}) custom-call(bf16[144,128,128]{2,1,0:T(8,128)(2,1)} %spectrum.1, s32[128,128]{1,0:T(8,128)} %land.1, f32[128,128]{1,0:T(8,128)} %speed.3, f32[128,128]{1,0:T(8,128)} %angle.3, ...), custom_call_target="tpu_custom_call" | custom-call | tf_op jit(solution)/shard_map/geo_halo/pallas_call | solution.py:386
  15.0 1.4 reduce_max.19
  17.0 199.5 %conditional.1 = ((f32[19760,128]{1,0:T(8,128)}, bf16[128,144,128]{2,1,0:T(8,128)(2,1)}, bf16[2,144,128]{2,1,0:T(8,128)(2,1)})) conditional(s32[]{:T(128)} %convert_element_type.63, (bf16[1152,1728]{0,1:T(8,128)(2,1)}, bf16[144,128,128]{2,1,0:T(8,128)(2,1)}, bf16[2,144,8,128]{3,2,1,0:T(8,128)(2,1)}, s32[128,128]{1,0:T(8,128)}, ...), branch_computations={%region_4.5_spmd, %region_5.6_spmd} | conditional | flops 24461180928 | bytes 11953184 | solution.py:1273
  17.0 1.1 copy.11.loss
  18.1 198.2 %advance_sea.1 = (f32[19760,128]{1,0:T(8,128)}, bf16[128,144,128]{2,1,0:T(8,128)(2,1)}, bf16[2,144,128]{2,1,0:T(8,128)(2,1)}) custom-call(bf16[144,128,128]{2,1,0:T(8,128)(2,1)} %get-tuple-element.53.spectrum, bf16[2,144,8,128]{3,2,1,0:T(8,128)(2,1)} %get-tuple-element.54.near, s32[128,128]{1,0:T(8,128)} %get-tuple-element.55.land, ...), custom_call_target="tpu_custom_call" | custom-call | flops 19874709504 | bytes 11943936 | tf_op jit(solution)/shard_map/cond/branch_1_fun/advance_sea/pallas_call | solution.py:1037
  216.5 15.5 %close.1 = bf16[144,128,128]{2,1,0:T(8,128)(2,1)} custom-call(f32[19760,128]{1,0:T(8,128)} %get-tuple-element.73.density, bf16[128,144,128]{2,1,0:T(8,128)(2,1)} %get-tuple-element.74.back, bf16[2,144,128]{2,1,0:T(8,128)(2,1)} %get-tuple-element.75.edge, f32[128,128]{1,0:T(8,128)} %speed.3, f32[2,8,128]{2,1,0:T(8,128)} %get-tuple-element.76.near_speed, ...), custom_call_target="tpu_custom_call" | custom-call | tf_op jit(solution)/shard_map/close/pallas_call | solution.py:1220
